TPU v7x, 32 devices: a whole 2x2x4 slice. The times are simulated.
32 devices in a mesh: grp: 2 (over y), seq: 8 (over z, x), head: 2 (over core).
Axes of the slice: x: 2, y: 2, z: 4, core: 2. Of those that a mesh axis runs over, the one named last changes fastest.
Arguments:
- queries: bfloat16 [2, 16, 64, 128], P(None, ('grp', 'seq'), 'head'), parts along dimension 1, may hold values from -1000 to 1000
- new_keys: bfloat16 [2, 16, 8, 128], P(None, ('grp', 'seq'), 'head'), parts along dimension 1, may hold values from -4 to 4
- token_value_rows: bfloat16 [2, 16, 8, 128], P(None, ('grp', 'seq'), 'head'), parts along dimension 1, may hold values from -6 to 6
- cache_keys: bfloat16 [2, 16, 16, 8, 128], P(None, 'grp', 'seq', 'head'), parts along dimension 1, may hold values from -6 to 6
- prefill_value_cache: bfloat16 [2, 16, 16, 8, 128], P(None, 'grp', 'seq', 'head'), parts along dimension 1, may hold values from -6 to 6
- lengths: int32 [16], P(('grp', 'seq')), parts along dimension 0, may hold values from 1 to 16, as said below
- slot_index: int32 [16], P('grp'), parts along dimension 0, may hold values from 0 to 7, as said below
- out_proj: bfloat16 [2, 8192, 8192], P(None, 'head', 'seq'), may hold values from -0.0625 to 0.0625
Outputs:
- attended: bfloat16 [2, 16, 8192], P(None, ('grp', 'head'), 'seq'), parts along dimension 1
There are 2 independent parts, one for each index of `grp`. A program takes and returns all parts, laid end to end along the dimension named above; an argument that names none is the same for every part. Nothing has to cross between parts.
Inputs may be any that keep to these rules, and one draw needn't show every extreme that they name: Decode sequence b reads prefill slot slot_index[b]; every slot is read by exactly one sequence. `lengths`: some sequence has all 16 positions.
All inputs are finite; a program needn't handle non-finite values.
Results may differ from a plain program's by a relative error of at most 0.008.
Values may be sent and summed in bfloat16 or wider, within the bound.
No kernel may reach another device: no remote copies, remote signals or barrier semaphores. Data moves between devices by JAX's collectives and lax.ppermute only.
A program may use at most 64 MiB of HBM per device.

v0:
```python
import jax
import jax.numpy as jnp
from jax import lax
from jax.sharding import PartitionSpec as P


def attend_layer(queried, key_rows, value_rows, key_new, value_new, lengths):
    row_count, kv_heads, head_dim = key_new.shape
    q_heads = queried.shape[1]
    grouped = queried.reshape(row_count, kv_heads, q_heads // kv_heads, head_dim)
    scaling = head_dim ** (-0.5)
    scores = (
        jnp.einsum("bgrd,btgd->bgrt", grouped, key_rows, preferred_element_type=jnp.float32)
        * scaling
    )
    allowed = lax.broadcasted_iota(jnp.int32, (row_count, key_rows.shape[1]), 1) < lengths[:, None]
    scores = jnp.where(allowed[:, None, None, :], scores, -1e30)
    own_score = (
        jnp.einsum("bgrd,bgd->bgr", grouped, key_new, preferred_element_type=jnp.float32) * scaling
    )
    peak_score = jnp.maximum(jnp.max(scores, axis=-1), own_score)
    raised = jnp.exp(scores - peak_score[..., None])
    own_raised = jnp.exp(own_score - peak_score)
    denominator = jnp.sum(raised, axis=-1) + own_raised
    weights = (raised / denominator[..., None]).astype(jnp.bfloat16)
    own_weight = (own_raised / denominator).astype(jnp.bfloat16)
    context = jnp.einsum("bgrt,btgd->bgrd", weights, value_rows, preferred_element_type=jnp.float32)
    context = (
        context
        + own_weight.astype(jnp.float32)[..., None] * value_new.astype(jnp.float32)[:, :, None, :]
    )
    return context.astype(jnp.bfloat16).reshape(row_count, q_heads * head_dim)


def local(
    queries,
    new_keys,
    token_value_rows,
    cache_keys,
    prefill_value_cache,
    lengths,
    slot_index,
    out_proj,
):
    picked_keys = jnp.take(cache_keys, slot_index, axis=1)
    picked_values = jnp.take(prefill_value_cache, slot_index, axis=1)
    layer_count = queries.shape[0]
    keys_all, values_all = (
        lax.all_to_all(picked_keys, "seq", split_axis=1, concat_axis=2, tiled=True),
        lax.all_to_all(picked_values, "seq", split_axis=1, concat_axis=2, tiled=True),
    )
    contexts = []
    for layer_idx in range(layer_count):
        key_rows = keys_all[layer_idx]
        value_rows = values_all[layer_idx]
        contexts.append(
            attend_layer(
                queries[layer_idx],
                key_rows,
                value_rows,
                new_keys[layer_idx],
                token_value_rows[layer_idx],
                lengths,
            )
        )
    partials = []
    for layer_idx in range(layer_count):
        weight_block = out_proj[layer_idx]
        partials.append(
            jnp.dot(
                lax.all_gather(contexts[layer_idx], "seq", axis=0, tiled=True),
                weight_block,
                preferred_element_type=jnp.float32,
            )
        )
    stacked = jnp.stack(partials)
    summed = lax.psum(stacked, "head")
    half_rows = summed.shape[1] // lax.axis_size("head")
    mine = lax.dynamic_slice_in_dim(summed, lax.axis_index("head") * half_rows, half_rows, 1)
    return mine.astype(jnp.bfloat16)


def solution(mesh):
    placed = (
        P(None, ("grp", "seq"), "head", None),
        P(None, ("grp", "seq"), "head", None),
        P(None, ("grp", "seq"), "head", None),
        P(None, "grp", "seq", "head", None),
        P(None, "grp", "seq", "head", None),
        P(("grp", "seq")),
        P("grp"),
        P(None, "head", "seq"),
    )
    return jax.shard_map(
        local,
        mesh=mesh,
        in_specs=placed,
        out_specs=P(None, ("grp", "head"), "seq"),
        check_vma=False,
    )
```

profile of v0, /device:TPU:0, one launch (start us, length us, event | category | flops | bytes accessed | tf_op | source)
XLA Modules:
  0.0 104.0 jit_solution(15908731956392144838)
XLA Ops:
  0.0 0.7 compare_and_fusion
  0.7 0.7 compare_select_fusion
  1.3 0.6 gather_fusion.1
  1.9 1.4 %gather_fusion = bf16[8,2,2,4,128]{4,3,2,1,0:T(4,128)(2,1)S(1)} fusion(bf16[2,8,2,4,128]{4,3,2,1,0:T(4,128)(2,1)} %param.13, s32[1024]{0:T(1024)S(1)} %pad_clamp_fusion), kind=kCustom, calls=%fused_computation.clone | custom fusion | bytes 65568 | tf_op jit(solution)/shard_map/jit(_take)/gather | solution.py:45
  3.3 0.7 select_bitcast_fusion.1
  4.0 7.3 %all-to-all-start = ((bf16[2,8,2,4,128]{4,3,2,0,1:T(4,128)(2,1)}), bf16[2,8,2,4,128]{4,3,2,0,1:T(4,128)(2,1)S(1)}, u32[]{:S(2)}, u32[]{:S(2)}) async-start(bf16[2,8,2,4,128]{4,3,2,0,1:T(4,128)(2,1)} %get-tuple-element.18), calls=%async_computation | async-start | bytes 65536 | tf_op jit(solution)/shard_map/all_to_all | solution.py:49
  11.9 0.7 slice_bitcast_fusion.1
  12.6 0.8 fusion.27
  13.5 0.8 fusion.24
  14.3 0.7 bitcast_convert_fusion.1
  15.0 3.0 %all-to-all-done = bf16[2,8,2,4,128]{4,3,2,0,1:T(4,128)(2,1)S(1)} async-done(((bf16[2,8,2,4,128]{4,3,2,0,1:T(4,128)(2,1)}), bf16[2,8,2,4,128]{4,3,2,0,1:T(4,128)(2,1)S(1)}, u32[]{:S(2)}, u32[]{:S(2)}) %all-to-all-start) | async-done | bytes 32800 | tf_op jit(solution)/shard_map/all_to_all | solution.py:49
  18.0 3.3 %all-to-all-start.1 = ((bf16[2,8,2,4,128]{4,3,2,0,1:T(4,128)(2,1)}), bf16[2,8,2,4,128]{4,3,2,0,1:T(4,128)(2,1)S(1)}, u32[]{:S(2)}, u32[]{:S(2)}) async-start(bf16[2,8,2,4,128]{4,3,2,0,1:T(4,128)(2,1)} %get-tuple-element.19), calls=%async_computation.1 | async-start | bytes 65536 | tf_op jit(solution)/shard_map/all_to_all | solution.py:50
  21.3 0.9 fusion.47
  22.3 0.2 fusion.22
  22.4 5.5 %all-to-all-done.1 = bf16[2,8,2,4,128]{4,3,2,0,1:T(4,128)(2,1)S(1)} async-done(((bf16[2,8,2,4,128]{4,3,2,0,1:T(4,128)(2,1)}), bf16[2,8,2,4,128]{4,3,2,0,1:T(4,128)(2,1)S(1)}, u32[]{:S(2)}, u32[]{:S(2)}) %all-to-all-start.1) | async-done | bytes 32800 | tf_op jit(solution)/shard_map/all_to_all | solution.py:50
  28.0 0.2 fusion.16
  28.2 0.9 fusion.46
  29.3 0.2 fusion.17
  29.5 30.5 %all-gather.1 = bf16[8,1,4096]{2,1,0:T(2,128)(2,1)S(1)} all-gather(bf16[1,1,4096]{2,1,0:T(2,128)(2,1)S(1)} %reshape.214), channel_id=1, replica_groups=mesh['grp'=2,'seq'=8,'head'=2] {'seq'}, dimensions={0}, use_global_device_ids=true | all-gather | bytes 73728 | tf_op jit(solution)/shard_map/all_gather | solution.py:71
  60.1 30.5 %all-gather = bf16[8,1,4096]{2,1,0:T(2,128)(2,1)S(1)} all-gather(bf16[1,1,4096]{2,1,0:T(2,128)(2,1)S(1)} %reshape.212), channel_id=1, replica_groups=mesh['grp'=2,'seq'=8,'head'=2] {'seq'}, dimensions={0}, use_global_device_ids=true | all-gather | bytes 73728 | tf_op jit(solution)/shard_map/all_gather | solution.py:71
  90.6 4.6 %fusion.9 = f32[1,8,1024]{2,1,0:T(8,128)S(1)} fusion(bf16[2,4096,1024]{2,1,0:T(8,128)(2,1)} %param.17, bf16[8,1,4096]{2,1,0:T(2,128)(2,1)S(1)} %all-gather.1), kind=kOutput, calls=%fused_computation.9 | convolution fusion | flops 67108864 | bytes 8486912 | tf_op jit(solution)/shard_map/dot_general | solution.py:70
  95.1 4.6 %fusion.6 = f32[1,8,1024]{2,1,0:T(8,128)S(1)} fusion(bf16[2,4096,1024]{2,1,0:T(8,128)(2,1)} %param.17, bf16[8,1,4096]{2,1,0:T(2,128)(2,1)S(1)} %all-gather), kind=kOutput, calls=%fused_computation.8 | convolution fusion | flops 67108864 | bytes 8486912 | tf_op jit(solution)/shard_map/dot_general | solution.py:70
  99.7 3.6 %psum.7 = bf16[2,8,1024]{2,1,0:T(8,128)(2,1)S(1)} all-reduce(f32[2,8,1024]{2,1,0:T(8,128)S(1)} %pad_maximum_fusion), channel_id=1, replica_groups=mesh['grp'=2,'seq'=8,'head'=2] {'head'}, use_global_device_ids=true, to_apply=%region_4.6 | all-reduce | flops 16384 | bytes 98304 | tf_op jit(solution)/shard_map/psum | solution.py:77
  103.3 0.6 dynamic-slice_convert_fusion
  (18 shorter events, 0.3 us)
Async XLA Ops:
  0.0 1.3 %copy-start = (bf16[2,8,2,4,128]{4,3,2,1,0:T(4,128)(2,1)S(1)}, bf16[2,8,2,4,128]{4,3,2,1,0:T(4,128)(2,1)}, u32[]{:S(2)}) copy-start(bf16[2,8,2,4,128]{4,3,2,1,0:T(4,128)(2,1)} %param.14) | copy-start | bytes 98308
  4.0 14.0 %all-to-all-start = ((bf16[2,8,2,4,128]{4,3,2,0,1:T(4,128)(2,1)}), bf16[2,8,2,4,128]{4,3,2,0,1:T(4,128)(2,1)S(1)}, u32[]{:S(2)}, u32[]{:S(2)}) async-start(bf16[2,8,2,4,128]{4,3,2,0,1:T(4,128)(2,1)} %get-tuple-element.18), calls=%async_computation | async-start | bytes 65536 | tf_op jit(solution)/shard_map/all_to_all | solution.py:49
  18.0 10.0 %all-to-all-start.1 = ((bf16[2,8,2,4,128]{4,3,2,0,1:T(4,128)(2,1)}), bf16[2,8,2,4,128]{4,3,2,0,1:T(4,128)(2,1)S(1)}, u32[]{:S(2)}, u32[]{:S(2)}) async-start(bf16[2,8,2,4,128]{4,3,2,0,1:T(4,128)(2,1)} %get-tuple-element.19), calls=%async_computation.1 | async-start | bytes 65536 | tf_op jit(solution)/shard_map/all_to_all | solution.py:50
where the time goes:
time: 105 us; the launch traced here: 104 us
  blocking collectives  64.6 us (62%)
  matrix products  13 us (12%)
  starting transfers between devices  10.6 us (10%)
  waiting for transfers between devices  8.49 us (8%)
  local copies, waits for them, and re-layouts  3.38 us (3%)
  other arithmetic  3.13 us (3%)
    all_gather x2, blocking collectives, local(): lax.all_gather(contexts[layer_idx], 'seq', axis=0, tiled=True)  61 us
    dot_general x2, matrix products, local(): jnp.dot(lax.all_gather(contexts[layer_idx], 'seq', axis=0, tiled=True), w...  9.15 us
    all_to_all x1, starting transfers between devices, local(): lax.all_to_all(picked_keys, 'seq', split_axis=1, concat_axis=2, tiled=True)  7.28 us
    all_to_all x1, waiting for transfers between devices, local(): lax.all_to_all(picked_values, 'seq', split_axis=1, concat_axis=2, tiled=T...  5.49 us
    psum x1, blocking collectives, local(): summed = lax.psum(stacked, 'head')  3.61 us
    all_to_all x1, starting transfers between devices, local(): lax.all_to_all(picked_values, 'seq', split_axis=1, concat_axis=2, tiled=T...  3.32 us
    all_to_all x1, waiting for transfers between devices, local(): lax.all_to_all(picked_keys, 'seq', split_axis=1, concat_axis=2, tiled=True)  3 us
  transfers between devices with their start and end apart: 2, of which 2 were waited for; matrix products, arithmetic and copies ran while one was open for 4% of the time, Pallas kernels for 0%

commit v1 on v0

v1 whole, which is shorter than its diff:
```python
import functools

import jax
import jax.numpy as jnp
from jax import lax
from jax.experimental import pallas as pl
from jax.experimental.pallas import tpu as pltpu
from jax.sharding import PartitionSpec as P

VMEM = pl.BlockSpec(memory_space=pltpu.VMEM)
SMEM = pl.BlockSpec(memory_space=pltpu.SMEM)
ANY = pl.BlockSpec(memory_space=pl.ANY)


def pick_kernel(slot_ref, keys_ref, values_ref, out_ref, sem):
    layers, rows = keys_ref.shape[0], keys_ref.shape[2]

    @pl.loop(0, out_ref.shape[0], unroll=out_ref.shape[0] <= 8)
    def _(b):
        slot = slot_ref[b]
        for which, source in enumerate((keys_ref, values_ref)):
            for layer in range(layers):
                pltpu.make_async_copy(
                    source.at[layer, slot],
                    out_ref.at[b, which, pl.ds(layer * rows, rows), :],
                    sem,
                ).start()

    pltpu.make_async_copy(out_ref, out_ref, sem).wait()


def attend_kernel(layers, kv_heads, len_ref, kv_ref, q_ref, new_key_ref, new_value_ref, out_ref):
    sources, _, block, depth = kv_ref.shape
    groups = layers * kv_heads
    positions = block // groups
    queries = q_ref[...]
    keys = kv_ref[:, 0].reshape(sources * block, depth)
    values = kv_ref[:, 1].reshape(sources * block, depth)
    scaling = depth ** (-0.5)
    scores = lax.dot_general(
        queries, keys, (((1,), (1,)), ((), ())), preferred_element_type=jnp.float32
    )
    per_group = queries.shape[0] // groups
    shape = (groups, per_group, sources * block)
    scores = scores.reshape(shape) * scaling
    group = lax.broadcasted_iota(jnp.int32, shape, 0)
    column = lax.broadcasted_iota(jnp.int32, shape, 2)
    within = column % block
    column_group = (within // (positions * kv_heads)) * kv_heads + within % kv_heads
    position = (column // block) * positions + (within // kv_heads) % positions
    allowed = (column_group == group) & (position < len_ref[0])
    scores = jnp.where(allowed, scores, -1e30)
    grouped = queries.astype(jnp.float32).reshape(groups, per_group, depth)
    new_key = new_key_ref[...].astype(jnp.float32)[:, None, :]
    own_score = jnp.sum(grouped * new_key, axis=-1, keepdims=True) * scaling
    peak = jnp.maximum(jnp.max(scores, axis=-1, keepdims=True), own_score)
    raised = jnp.exp(scores - peak)
    own_raised = jnp.exp(own_score - peak)
    denominator = jnp.sum(raised, axis=-1, keepdims=True) + own_raised
    weights = (raised / denominator).astype(jnp.bfloat16)
    own_weight = (own_raised / denominator).astype(jnp.bfloat16)
    context = jnp.dot(
        weights.reshape(groups * per_group, sources * block),
        values,
        preferred_element_type=jnp.float32,
    ).reshape(groups, per_group, depth)
    new_value = new_value_ref[...].astype(jnp.float32)[:, None, :]
    context = context + own_weight.astype(jnp.float32) * new_value
    context = context.astype(jnp.bfloat16).reshape(groups * per_group, depth)
    out_ref[...] = jnp.broadcast_to(context[None], out_ref.shape)


def project_kernel(
    chunk, head_ref, context_ref, weight_ref, mine_ref, other_ref, wide, held, sems
):
    layers, depth_rows, columns = weight_ref.shape
    sequences, rows, depth = context_ref.shape
    heads = rows // layers
    chunks = depth_rows // chunk
    copies = []
    for layer in range(layers):
        for c in range(chunks):
            copies.append(
                pltpu.make_async_copy(
                    weight_ref.at[layer, pl.ds(c * chunk, chunk), :],
                    held.at[layer, pl.ds(c * chunk, chunk), :],
                    sems.at[layer, c],
                )
            )
            copies[-1].start()
    wide[...] = context_ref[...].astype(jnp.float32).reshape(sequences * rows, depth)
    heads_per_chunk = chunk // depth
    half = sequences // 2
    first = head_ref[0] == 0
    for layer in range(layers):
        total = jnp.zeros((sequences, columns), jnp.float32)
        for c in range(chunks):
            lhs = jnp.concatenate(
                [
                    wide[pl.ds(layer * heads + c * heads_per_chunk + h, sequences, stride=rows), :]
                    for h in range(heads_per_chunk)
                ],
                axis=1,
            ).astype(jnp.bfloat16)
            copies[layer * chunks + c].wait()
            total += jnp.dot(
                lhs,
                held[layer, c * chunk : (c + 1) * chunk, :],
                preferred_element_type=jnp.float32,
            )
        low, high = total[:half], total[half:]
        mine_ref[layer] = jnp.where(first, low, high)
        other_ref[layer] = jnp.where(first, high, low)


def local(
    queries,
    new_keys,
    token_value_rows,
    cache_keys,
    prefill_value_cache,
    lengths,
    slot_index,
    out_proj,
):
    layers, _, heads, depth = queries.shape
    kv_heads = new_keys.shape[2]
    _, sequences, positions, _, _ = cache_keys.shape
    columns = out_proj.shape[2]
    bf16, f32 = jnp.bfloat16, jnp.float32
    flat = (layers, sequences, positions * kv_heads, depth)
    block = layers * positions * kv_heads
    picked = pl.pallas_call(
        pick_kernel,
        out_shape=jax.ShapeDtypeStruct((sequences, 2, block, depth), bf16),
        in_specs=[SMEM, ANY, ANY],
        out_specs=VMEM,
        scratch_shapes=[pltpu.SemaphoreType.DMA],
        compiler_params=pltpu.CompilerParams(vmem_limit_bytes=8 * 2**20),
    )(slot_index, cache_keys.reshape(flat), prefill_value_cache.reshape(flat))
    gathered = lax.all_to_all(picked, "seq", 0, 0, tiled=True)
    contexts = pl.pallas_call(
        functools.partial(attend_kernel, layers, kv_heads),
        out_shape=jax.ShapeDtypeStruct((sequences, layers * heads, depth), bf16),
        in_specs=[SMEM, VMEM, VMEM, VMEM, VMEM],
        out_specs=VMEM,
        compiler_params=pltpu.CompilerParams(vmem_limit_bytes=24 * 2**20),
    )(
        lengths,
        gathered,
        queries.reshape(layers * heads, depth),
        new_keys.reshape(layers * kv_heads, depth),
        token_value_rows.reshape(layers * kv_heads, depth),
    )
    contexts = lax.all_to_all(contexts, "seq", 0, 0, tiled=True)
    half = sequences // lax.axis_size("head")
    chunk = 4 * depth
    part = jax.ShapeDtypeStruct((layers, half, columns), f32)
    mine, other = pl.pallas_call(
        functools.partial(project_kernel, chunk),
        out_shape=(part, part),
        in_specs=[SMEM, VMEM, ANY],
        out_specs=(VMEM, VMEM),
        scratch_shapes=[
            pltpu.VMEM((sequences * layers * heads, depth), f32),
            pltpu.VMEM(out_proj.shape, bf16),
            pltpu.SemaphoreType.DMA((layers, heads * depth // chunk)),
        ],
        compiler_params=pltpu.CompilerParams(vmem_limit_bytes=40 * 2**20),
    )(lax.axis_index("head").reshape(1), contexts, out_proj)
    arrived = lax.ppermute(other, "head", [(0, 1), (1, 0)])
    return (mine + arrived).astype(bf16)


def solution(mesh):
    placed = (
        P(None, ("grp", "seq"), "head", None),
        P(None, ("grp", "seq"), "head", None),
        P(None, ("grp", "seq"), "head", None),
        P(None, "grp", "seq", "head", None),
        P(None, "grp", "seq", "head", None),
        P(("grp", "seq")),
        P("grp"),
        P(None, "head", "seq"),
    )
    return jax.shard_map(
        local,
        mesh=mesh,
        in_specs=placed,
        out_specs=P(None, ("grp", "head"), "seq"),
        check_vma=False,
    )
```

time: 105 us -> 40.1 us (0.38)
  blocking collectives: 64.6 us -> 0 us
  matrix products: 13 us -> 0 us
  Pallas kernels: 0 us -> 8.51 us
  waiting for transfers between devices: 8.49 us -> 14.7 us
  other arithmetic: 3.13 us -> 0.62 us
    all_gather x2 -> x0, blocking collectives: 61 us -> none  [local(): lax.all_gather(contexts[layer_idx], 'seq', axis=0, tiled=True)]
    dot_general x8 -> x0, matrix products: 13 us -> none  [the longest x2 9.15 us: local(): jnp.dot(lax.all_gather(contexts[layer_idx], 'seq', axis=0, tiled=True), w...]
    pallas_call x0 -> x3, Pallas kernels: none -> 8.51 us  [the longest x1 6.19 us: local(): pl.pallas_call(functools.partial(project_kernel, chunk), out_shape=(part,...]
    all_to_all x2, waiting for transfers between devices: 8.49 us -> 13.5 us  [the longest x1 7.28 us: local(): contexts = lax.all_to_all(contexts, 'seq', 0, 0, tiled=True)]
    unnamed x4 -> x12, local copies, waits for them, and re-layouts: 0.03 us -> 4.25 us
    psum x1 -> x0, blocking collectives: 3.61 us -> none  [local(): summed = lax.psum(stacked, 'head')]
    gather x2 -> x0, local copies, waits for them, and re-layouts: 1.94 us -> none  [the longest x1 1.35 us: local(): picked_keys = jnp.take(cache_keys, slot_index, axis=1)]
    select_n x2 -> x0, other arithmetic: 1.38 us -> none  [local(): picked_keys = jnp.take(cache_keys, slot_index, axis=1)]
  transfers between devices with their start and end apart: 2 -> 3, of which waited for: 2 -> 3; matrix products, arithmetic and copies ran while one was open for 4% -> 0% of each run, Pallas kernels for 0% -> 0%
where the time goes in v1:
time: 40.1 us; the launch traced here: 39.5 us
  waiting for transfers between devices  14.7 us (37%)
  starting transfers between devices  10.7 us (27%)
  Pallas kernels  8.51 us (21%)
  local copies, waits for them, and re-layouts  4.25 us (11%)
  between operations  0.7 us (2%)
  other arithmetic  0.62 us (2%)
    all_to_all x1, starting transfers between devices, local(): gathered = lax.all_to_all(picked, 'seq', 0, 0, tiled=True)  7.29 us
    all_to_all x1, waiting for transfers between devices, local(): contexts = lax.all_to_all(contexts, 'seq', 0, 0, tiled=True)  7.28 us
    all_to_all x1, waiting for transfers between devices, local(): gathered = lax.all_to_all(picked, 'seq', 0, 0, tiled=True)  6.25 us
    pallas_call x1, Pallas kernels, local(): pl.pallas_call(functools.partial(project_kernel, chunk), out_shape=(part,...  6.19 us
    unnamed x12, local copies, waits for them, and re-layouts  4.25 us
    all_to_all x1, starting transfers between devices, local(): contexts = lax.all_to_all(contexts, 'seq', 0, 0, tiled=True)  3.37 us
    pallas_call x1, Pallas kernels, local(): pl.pallas_call(pick_kernel, out_shape=jax.ShapeDtypeStruct((sequences, 2,...  1.24 us
    ppermute x1, waiting for transfers between devices, local(): arrived = lax.ppermute(other, 'head', [(0, 1), (1, 0)])  1.19 us
  transfers between devices with their start and end apart: 3, of which 3 were waited for; matrix products, arithmetic and copies ran while one was open for 0% of the time, Pallas kernels for 0%

profile of v1, /device:TPU:0, one launch (start us, length us, event | category | flops | bytes accessed | tf_op | source)
XLA Modules:
  0.0 39.5 jit_solution(13684661373942540834)
XLA Ops:
  0.0 0.0 copy-start
  0.0 0.8 %copy-done = bf16[2,8,2,4,128]{4,3,2,1,0:T(4,128)(2,1)S(1)} copy-done((bf16[2,8,2,4,128]{4,3,2,1,0:T(4,128)(2,1)S(1)}, bf16[2,8,2,4,128]{4,3,2,1,0:T(4,128)(2,1)}, u32[]{:S(2)}) %copy-start) | copy-done | bytes 32792
  0.8 0.0 copy-start.1
  0.8 0.8 %copy-done.1 = bf16[2,8,2,4,128]{4,3,2,1,0:T(4,128)(2,1)S(1)} copy-done((bf16[2,8,2,4,128]{4,3,2,1,0:T(4,128)(2,1)S(1)}, bf16[2,8,2,4,128]{4,3,2,1,0:T(4,128)(2,1)}, u32[]{:S(2)}) %copy-start.1) | copy-done | bytes 32792
  1.5 0.0 copy-start.5
  1.5 0.7 %copy-done.5 = s32[8]{0:T(128)S(1)} copy-done((s32[8]{0:T(128)S(1)}, s32[8]{0:T(128)}, u32[]{:S(2)}) %copy-start.5) | copy-done | bytes 56
  2.2 1.2 %shard_map.82 = bf16[8,2,16,128]{3,2,1,0:T(8,128)(2,1)} custom-call(s32[8]{0:T(128)S(1)} %copy-done.5, bf16[2,8,8,128]{3,2,1,0:T(8,128)(2,1)S(1)} %bitcast.6, bf16[2,8,8,128]{3,2,1,0:T(8,128)(2,1)S(1)} %bitcast.7), custom_call_target="tpu_custom_call" | custom-call | tf_op jit(solution)/shard_map/pallas_call | solution.py:133
  3.4 7.3 %all-to-all-start = ((bf16[8,2,16,128]{3,2,1,0:T(8,128)(2,1)}), bf16[8,2,16,128]{3,2,1,0:T(8,128)(2,1)S(1)}, u32[]{:S(2)}, u32[]{:S(2)}) async-start(bf16[8,2,16,128]{3,2,1,0:T(8,128)(2,1)} %shard_map.82), calls=%async_computation | async-start | bytes 131072 | tf_op jit(solution)/shard_map/all_to_all | solution.py:141
  11.4 6.3 %all-to-all-done.kv_ref = bf16[8,2,16,128]{3,2,1,0:T(8,128)(2,1)S(1)} async-done(((bf16[8,2,16,128]{3,2,1,0:T(8,128)(2,1)}), bf16[8,2,16,128]{3,2,1,0:T(8,128)(2,1)S(1)}, u32[]{:S(2)}, u32[]{:S(2)}) %all-to-all-start) | async-done | bytes 65568 | tf_op jit(solution)/shard_map/all_to_all | solution.py:141
  17.6 0.0 copy-start.2
  17.6 0.7 %copy-done.2 = bf16[2,1,32,128]{3,2,1,0:T(8,128)(2,1)S(1)} copy-done((bf16[2,1,32,128]{3,2,1,0:T(8,128)(2,1)S(1)}, bf16[2,1,32,128]{3,2,1,0:T(8,128)(2,1)}, u32[]{:S(2)}) %copy-start.2) | copy-done | bytes 16408
  18.3 0.0 copy-start.3
  18.3 0.7 %copy-done.3 = bf16[2,1,4,128]{3,2,1,0:T(4,128)(2,1)S(1)} copy-done((bf16[2,1,4,128]{3,2,1,0:T(4,128)(2,1)S(1)}, bf16[2,1,4,128]{3,2,1,0:T(4,128)(2,1)}, u32[]{:S(2)}) %copy-start.3) | copy-done | bytes 2072
  19.0 0.0 copy-start.4
  19.0 0.7 %copy-done.4 = bf16[2,1,4,128]{3,2,1,0:T(4,128)(2,1)S(1)} copy-done((bf16[2,1,4,128]{3,2,1,0:T(4,128)(2,1)S(1)}, bf16[2,1,4,128]{3,2,1,0:T(4,128)(2,1)}, u32[]{:S(2)}) %copy-start.4) | copy-done | bytes 2072
  19.7 1.1 %shard_map.83 = bf16[8,64,128]{2,1,0:T(8,128)(2,1)} custom-call(s32[1]{0:T(128)S(6)} %copy.9.len_ref, bf16[8,2,16,128]{3,2,1,0:T(8,128)(2,1)S(1)} %all-to-all-done.kv_ref, bf16[64,128]{1,0:T(8,128)(2,1)S(1)} %bitcast.8, bf16[8,128]{1,0:T(8,128)(2,1)S(1)} %bitcast.9, bf16[8,128]{1,0:T(8,128)(2,1)S(1)} %bitcast.10), custom_call_target="tpu_custom_call" | custom-call | tf_op jit(solution)/shard_map/pallas_call | solution.py:142
  20.8 3.4 %all-to-all-start.1 = ((bf16[8,64,128]{2,1,0:T(8,128)(2,1)}), bf16[8,64,128]{2,1,0:T(8,128)(2,1)S(1)}, u32[]{:S(2)}, u32[]{:S(2)}) async-start(bf16[8,64,128]{2,1,0:T(8,128)(2,1)} %shard_map.83), calls=%async_computation.1 | async-start | bytes 262144 | tf_op jit(solution)/shard_map/all_to_all | solution.py:155
  24.2 7.3 %all-to-all-done.1.context_ref = bf16[8,64,128]{2,1,0:T(8,128)(2,1)S(1)} async-done(((bf16[8,64,128]{2,1,0:T(8,128)(2,1)}), bf16[8,64,128]{2,1,0:T(8,128)(2,1)S(1)}, u32[]{:S(2)}, u32[]{:S(2)}) %all-to-all-start.1) | async-done | bytes 131104 | tf_op jit(solution)/shard_map/all_to_all | solution.py:155
  31.4 6.2 %shard_map.84 = (f32[2,4,1024]{2,1,0:T(4,128)S(1)}, f32[2,4,1024]{2,1,0:T(4,128)S(1)}) custom-call(s32[1]{0:T(128)} %bitcast.head_ref, bf16[8,64,128]{2,1,0:T(8,128)(2,1)S(1)} %all-to-all-done.1.context_ref, bf16[2,4096,1024]{2,1,0:T(8,128)(2,1)} %weight_ref.1), custom_call_target="tpu_custom_call" | custom-call | tf_op jit(solution)/shard_map/pallas_call | solution.py:159
  37.6 0.1 collective-permute-start
  37.7 1.2 %collective-permute-done = f32[2,4,1024]{2,1,0:T(4,128)S(1)} collective-permute-done((f32[2,4,1024]{2,1,0:T(4,128)S(1)}, f32[2,4,1024]{2,1,0:T(4,128)S(1)}, u32[]{:S(2)}, u32[]{:S(2)}) %collective-permute-start) | collective-permute-done | bytes 32800 | tf_op jit(solution)/shard_map/ppermute | solution.py:171
  38.9 0.6 %add_convert_fusion = bf16[2,4,1024]{2,1,0:T(4,128)(2,1)} fusion(f32[2,4,1024]{2,1,0:T(4,128)S(1)} %get-tuple-element.7, f32[2,4,1024]{2,1,0:T(4,128)S(1)} %collective-permute-done), kind=kLoop, calls=%fused_computation | loop fusion | flops 16384 | bytes 81920 | tf_op jit(solution)/shard_map/convert_element_type | solution.py:172
Async XLA Ops:
  0.0 0.8 %copy-start = (bf16[2,8,2,4,128]{4,3,2,1,0:T(4,128)(2,1)S(1)}, bf16[2,8,2,4,128]{4,3,2,1,0:T(4,128)(2,1)}, u32[]{:S(2)}) copy-start(bf16[2,8,2,4,128]{4,3,2,1,0:T(4,128)(2,1)} %param.11) | copy-start | bytes 98308
  0.8 0.8 %copy-start.1 = (bf16[2,8,2,4,128]{4,3,2,1,0:T(4,128)(2,1)S(1)}, bf16[2,8,2,4,128]{4,3,2,1,0:T(4,128)(2,1)}, u32[]{:S(2)}) copy-start(bf16[2,8,2,4,128]{4,3,2,1,0:T(4,128)(2,1)} %param.12) | copy-start | bytes 98308
  1.5 0.7 %copy-start.5 = (s32[8]{0:T(128)S(1)}, s32[8]{0:T(128)}, u32[]{:S(2)}) copy-start(s32[8]{0:T(128)} %slot_ref.1) | copy-start | bytes 100
  3.4 14.2 %all-to-all-start = ((bf16[8,2,16,128]{3,2,1,0:T(8,128)(2,1)}), bf16[8,2,16,128]{3,2,1,0:T(8,128)(2,1)S(1)}, u32[]{:S(2)}, u32[]{:S(2)}) async-start(bf16[8,2,16,128]{3,2,1,0:T(8,128)(2,1)} %shard_map.82), calls=%async_computation | async-start | bytes 131072 | tf_op jit(solution)/shard_map/all_to_all | solution.py:141
  17.6 0.7 %copy-start.2 = (bf16[2,1,32,128]{3,2,1,0:T(8,128)(2,1)S(1)}, bf16[2,1,32,128]{3,2,1,0:T(8,128)(2,1)}, u32[]{:S(2)}) copy-start(bf16[2,1,32,128]{3,2,1,0:T(8,128)(2,1)} %param.8) | copy-start | bytes 49156
  18.3 0.7 %copy-start.3 = (bf16[2,1,4,128]{3,2,1,0:T(4,128)(2,1)S(1)}, bf16[2,1,4,128]{3,2,1,0:T(4,128)(2,1)}, u32[]{:S(2)}) copy-start(bf16[2,1,4,128]{3,2,1,0:T(4,128)(2,1)} %param.9) | copy-start | bytes 6148
  19.0 0.7 %copy-start.4 = (bf16[2,1,4,128]{3,2,1,0:T(4,128)(2,1)S(1)}, bf16[2,1,4,128]{3,2,1,0:T(4,128)(2,1)}, u32[]{:S(2)}) copy-start(bf16[2,1,4,128]{3,2,1,0:T(4,128)(2,1)} %param.10) | copy-start | bytes 6148
  20.8 10.7 %all-to-all-start.1 = ((bf16[8,64,128]{2,1,0:T(8,128)(2,1)}), bf16[8,64,128]{2,1,0:T(8,128)(2,1)S(1)}, u32[]{:S(2)}, u32[]{:S(2)}) async-start(bf16[8,64,128]{2,1,0:T(8,128)(2,1)} %shard_map.83), calls=%async_computation.1 | async-start | bytes 262144 | tf_op jit(solution)/shard_map/all_to_all | solution.py:155
  37.6 1.3 %collective-permute-start = (f32[2,4,1024]{2,1,0:T(4,128)S(1)}, f32[2,4,1024]{2,1,0:T(4,128)S(1)}, u32[]{:S(2)}, u32[]{:S(2)}) collective-permute-start(f32[2,4,1024]{2,1,0:T(4,128)S(1)} %get-tuple-element.8), channel_id=1, source_target_pairs={{0,1},{1,0},{2,3},{3,2},{4,5},{5,4},{6,7},{7,6},{8,9},{9,8},{10,11... | collective-permute-start | bytes 98312 | tf_op jit(solution)/shard_map/ppermute | solution.py:171

commit v2 on v1

--- a/solution.py
+++ b/solution.py
@@ -10,6 +10,9 @@
 VMEM = pl.BlockSpec(memory_space=pltpu.VMEM)
 SMEM = pl.BlockSpec(memory_space=pltpu.SMEM)
 ANY = pl.BlockSpec(memory_space=pl.ANY)
+HBM = pl.BlockSpec(memory_space=pltpu.HBM)
+MIB = 2**20
+COVER = pl.CostEstimate(flops=10**10, bytes_accessed=2**20, transcendentals=0)
 
 
 def pick_kernel(slot_ref, keys_ref, values_ref, out_ref, sem):
@@ -113,7 +116,281 @@
         other_ref[layer] = jnp.where(first, high, low)
 
 
-def local(
+def softmax_context(queries, new_keys, new_values, keys, values, allowed, groups):
+    rows, depth = queries.shape
+    grouped = (groups, rows // groups, depth)
+    scaling = depth ** (-0.5)
+    scores = lax.dot_general(
+        queries, keys, (((1,), (1,)), ((), ())), preferred_element_type=jnp.float32
+    )
+    scores = jnp.where(allowed, scores.reshape(allowed.shape) * scaling, -1e30)
+    new_keys = new_keys.astype(jnp.float32)[:, None, :]
+    own_score = jnp.sum(
+        queries.astype(jnp.float32).reshape(grouped) * new_keys, axis=-1, keepdims=True
+    )
+    own_score = own_score * scaling
+    peak = jnp.maximum(jnp.max(scores, axis=-1, keepdims=True), own_score)
+    raised = jnp.exp(scores - peak)
+    own_raised = jnp.exp(own_score - peak)
+    denominator = jnp.sum(raised, axis=-1, keepdims=True) + own_raised
+    weights = (raised / denominator).astype(jnp.bfloat16)
+    own_weight = (own_raised / denominator).astype(jnp.bfloat16)
+    context = jnp.dot(
+        weights.reshape(rows, keys.shape[0]), values, preferred_element_type=jnp.float32
+    ).reshape(grouped)
+    new_values = new_values.astype(jnp.float32)[:, None, :]
+    context = context + own_weight.astype(jnp.float32) * new_values
+    return context.astype(jnp.bfloat16).reshape(rows, depth)
+
+
+def place():
+    index = lax.axis_index("seq")
+    return index // 2, index % 2
+
+
+def stage_kernel(
+    pairs,
+    len_ref,
+    slot_hbm,
+    keys_hbm,
+    values_hbm,
+    queries_hbm,
+    new_keys_hbm,
+    new_values_hbm,
+    *refs,
+):
+    blocks, side_ref = refs[:pairs], refs[pairs]
+    slots, keys, values, sem = refs[pairs + 1 :]
+    layers, _, rows, _ = keys.shape
+    query_rows, new_rows = queries_hbm.shape[0], new_keys_hbm.shape[0]
+    sources = (slot_hbm, keys_hbm, values_hbm, queries_hbm, new_keys_hbm, new_values_hbm)
+    targets = (
+        slots,
+        keys,
+        values,
+        side_ref.at[pl.ds(0, query_rows)],
+        side_ref.at[pl.ds(query_rows, new_rows)],
+        side_ref.at[pl.ds(query_rows + new_rows, new_rows)],
+    )
+    copies = [
+        pltpu.make_async_copy(source, target, sem.at[i])
+        for i, (source, target) in enumerate(zip(sources, targets, strict=True))
+    ]
+    for copy in copies:
+        copy.start()
+    for copy in copies:
+        copy.wait()
+    tail = query_rows + 2 * new_rows
+    length = len_ref[0].astype(jnp.float32)
+    side_ref[tail:, :] = jnp.full((side_ref.shape[0] - tail, side_ref.shape[1]), length).astype(
+        jnp.bfloat16
+    )
+    pair, _ = place()
+    for k in range(pairs):
+        for side in range(2):
+            slot = slots[(pair ^ k) * 2 + side]
+            for which, held in enumerate((keys, values)):
+                for layer in range(layers):
+                    blocks[k][side, which, layer * rows : (layer + 1) * rows, :] = held[layer, slot]
+
+
+def pack_kernel(*refs):
+    start = 0
+    for ref in refs[:-1]:
+        rows = ref[...].reshape(-1, ref.shape[-1])
+        refs[-1][start : start + rows.shape[0], :] = rows
+        start += rows.shape[0]
+
+
+def pair_attend_kernel(pairs, layers, kv_heads, query_rows, *refs):
+    blocks, side_ref, partner_ref, out_ref = refs[:pairs], refs[pairs], refs[pairs + 1], refs[-1]
+    pair, mine = place()
+    _, _, block, depth = blocks[0].shape
+    groups = layers * kv_heads
+    positions = block // groups
+    per_block = 4 * block
+    sources = 2 * pairs
+    shape = (groups, query_rows // groups, sources * block)
+    group = lax.broadcasted_iota(jnp.int32, shape, 0)
+    column = lax.broadcasted_iota(jnp.int32, shape, 2)
+    within = column % block
+    column_group = (within // (positions * kv_heads)) * kv_heads + within % kv_heads
+    source = column // block
+    source = ((source % pairs) ^ pair) * 2 + ((source // pairs) ^ mine)
+    position = source * positions + (within // kv_heads) % positions
+    same_group = column_group == group
+    tail = pairs * per_block
+
+    def side_rows(sequence, first, count):
+        here = side_ref[first : first + count, :]
+        there = partner_ref[tail + first : tail + first + count, :]
+        return jnp.where(mine == sequence, here, there)
+
+    for sequence in range(2):
+        stacked = []
+        for which in range(2):
+            first = (sequence * 2 + which) * block
+            stacked.append(
+                jnp.concatenate(
+                    [ref[sequence, which] for ref in blocks]
+                    + [
+                        partner_ref[k * per_block + first : k * per_block + first + block, :]
+                        for k in range(pairs)
+                    ],
+                    axis=0,
+                )
+            )
+        queries = side_rows(sequence, 0, query_rows)
+        new_keys = side_rows(sequence, query_rows, groups)
+        new_values = side_rows(sequence, query_rows + groups, groups)
+        length = side_rows(sequence, query_rows + 2 * groups, 16)[:1, :1].astype(jnp.float32)
+        allowed = same_group & (position.astype(jnp.float32) < length[None])
+        out_ref[sequence] = softmax_context(
+            queries, new_keys, new_values, stacked[0], stacked[1], allowed, groups
+        )
+
+
+def pair_project_kernel(pairs, layers, chunk, *refs):
+    contexts, weight_ref, mine_ref, other_ref, wide = refs[:pairs], *refs[pairs:]
+    _, rows, depth = contexts[0].shape
+    heads = rows // layers
+    sequences = 2 * pairs
+    columns = weight_ref.shape[2]
+    for k in range(pairs):
+        wide[k * 2 * rows : (k + 1) * 2 * rows, :] = (
+            contexts[k][...].astype(jnp.float32).reshape(2 * rows, depth)
+        )
+    heads_per_chunk = chunk // depth
+    half = sequences // 2
+    pair, _ = place()
+    first = lax.axis_index("head") == 0
+    for layer in range(layers):
+        total = jnp.zeros((sequences, columns), jnp.float32)
+        for c in range(heads // heads_per_chunk):
+            lhs = jnp.concatenate(
+                [
+                    wide[pl.ds(layer * heads + c * heads_per_chunk + h, sequences, stride=rows), :]
+                    for h in range(heads_per_chunk)
+                ],
+                axis=1,
+            ).astype(jnp.bfloat16)
+            total += jnp.dot(
+                lhs,
+                weight_ref[layer, c * chunk : (c + 1) * chunk, :],
+                preferred_element_type=jnp.float32,
+            )
+        bit = 1
+        while bit < pairs:
+            span = 2 * bit
+            swapped = jnp.concatenate(
+                [
+                    total[(j ^ 1) * span : (j ^ 1) * span + span]
+                    for j in range(sequences // span)
+                ],
+                axis=0,
+            )
+            total = jnp.where((pair & bit) != 0, swapped, total)
+            bit *= 2
+        low, high = total[:half], total[half:]
+        mine_ref[layer] = jnp.where(first, low, high)
+        other_ref[layer] = jnp.where(first, high, low)
+
+
+def exchange(blocks):
+    count = 2 * len(blocks)
+    return [blocks[0]] + [
+        lax.ppermute(block, "seq", [(i, i ^ (2 * k)) for i in range(count)])
+        for k, block in enumerate(blocks)
+        if k
+    ]
+
+
+def params(limit):
+    return pltpu.CompilerParams(vmem_limit_bytes=limit * MIB)
+
+
+def in_hbm(*arrays):
+    return [pltpu.with_memory_space_constraint(array, pltpu.HBM) for array in arrays]
+
+
+def by_pairs(
+    queries,
+    new_keys,
+    token_value_rows,
+    cache_keys,
+    prefill_value_cache,
+    lengths,
+    slot_index,
+    out_proj,
+):
+    layers, _, heads, depth = queries.shape
+    kv_heads = new_keys.shape[2]
+    _, sequences, positions, _, _ = cache_keys.shape
+    columns = out_proj.shape[2]
+    pairs = sequences // 2
+    bf16, f32 = jnp.bfloat16, jnp.float32
+    flat = (layers, sequences, positions * kv_heads, depth)
+    block = layers * positions * kv_heads
+    query_rows, groups = layers * heads, layers * kv_heads
+    side_rows = query_rows + 2 * groups + 16
+    block_shape = jax.ShapeDtypeStruct((2, 2, block, depth), bf16)
+    *blocks, side = pl.pallas_call(
+        functools.partial(stage_kernel, pairs),
+        out_shape=[block_shape] * pairs + [jax.ShapeDtypeStruct((side_rows, depth), bf16)],
+        in_specs=[SMEM] + [HBM] * 6,
+        out_specs=[VMEM] * (pairs + 1),
+        scratch_shapes=[
+            pltpu.SMEM((sequences,), jnp.int32),
+            pltpu.VMEM(flat, bf16),
+            pltpu.VMEM(flat, bf16),
+            pltpu.SemaphoreType.DMA((6,)),
+        ],
+        compiler_params=params(4),
+        cost_estimate=COVER,
+    )(
+        lengths,
+        *in_hbm(
+            slot_index,
+            cache_keys.reshape(flat),
+            prefill_value_cache.reshape(flat),
+            queries.reshape(query_rows, depth),
+            new_keys.reshape(groups, depth),
+            token_value_rows.reshape(groups, depth),
+        ),
+    )
+    blocks = exchange(blocks)
+    packed = pl.pallas_call(
+        pack_kernel,
+        out_shape=jax.ShapeDtypeStruct((pairs * 4 * block + side_rows, depth), bf16),
+        in_specs=[VMEM] * (pairs + 1),
+        out_specs=VMEM,
+        compiler_params=params(4),
+        cost_estimate=COVER,
+    )(*blocks, side)
+    partner = lax.ppermute(packed, "seq", [(i, i ^ 1) for i in range(sequences)])
+    contexts = pl.pallas_call(
+        functools.partial(pair_attend_kernel, pairs, layers, kv_heads, query_rows),
+        out_shape=jax.ShapeDtypeStruct((2, query_rows, depth), bf16),
+        in_specs=[VMEM] * (pairs + 2),
+        out_specs=VMEM,
+        compiler_params=params(4),
+        cost_estimate=COVER,
+    )(*blocks, side, partner)
+    contexts = exchange([contexts] * pairs)
+    part = jax.ShapeDtypeStruct((layers, sequences // 2, columns), f32)
+    mine, other = pl.pallas_call(
+        functools.partial(pair_project_kernel, pairs, layers, 4 * depth),
+        out_shape=(part, part),
+        in_specs=[VMEM] * (pairs + 1),
+        out_specs=(VMEM, VMEM),
+        scratch_shapes=[pltpu.VMEM((sequences * query_rows, depth), f32)],
+        compiler_params=params(24),
+    )(*contexts, out_proj)
+    arrived = lax.ppermute(other, "head", [(0, 1), (1, 0)])
+    return (mine + arrived).astype(bf16)
+
+
+def by_all_to_all(
     queries,
     new_keys,
     token_value_rows,
@@ -183,8 +460,10 @@
         P("grp"),
         P(None, "head", "seq"),
     )
+    seq = mesh.shape["seq"]
+    few = seq in (2, 4, 8)
     return jax.shard_map(
-        local,
+        by_pairs if few else by_all_to_all,
         mesh=mesh,
         in_specs=placed,
         out_specs=P(None, ("grp", "head"), "seq"),

time: 40.1 us -> 28.9 us (0.72)
  Pallas kernels: 8.51 us -> 3.91 us
  local copies, waits for them, and re-layouts: 4.25 us -> 0.02 us
  waiting for transfers between devices: 14.7 us -> 11.7 us
  starting transfers between devices: 10.7 us -> 11.8 us
    all_to_all x2 -> x0, waiting for transfers between devices: 13.5 us -> none  [the longest x1 7.28 us: local(): contexts = lax.all_to_all(contexts, 'seq', 0, 0, tiled=True)]
    ppermute x1 -> x8, starting transfers between devices: 0.07 us -> 11.8 us  [the longest x6 10.1 us: exchange(): lax.ppermute(block, 'seq', [(i, i ^ 2 * k) for i in range(count)])]
    all_to_all x2 -> x0, starting transfers between devices: 10.7 us -> none  [the longest x1 7.29 us: local(): gathered = lax.all_to_all(picked, 'seq', 0, 0, tiled=True)]
    ppermute x1 -> x8, waiting for transfers between devices: 1.19 us -> 11.7 us  [the longest x6 7.42 us: exchange(): lax.ppermute(block, 'seq', [(i, i ^ 2 * k) for i in range(count)])]
    pallas_call x3 -> x4, Pallas kernels: 8.51 us -> 3.91 us  [the longest x1 2.28 us: by_pairs(): pl.pallas_call(functools.partial(pair_project_kernel, pairs, layers, 4 *...]
    unnamed x12 -> x8, local copies, waits for them, and re-layouts: 4.25 us -> 0.02 us
  transfers between devices with their start and end apart: 3 -> 8, of which waited for: 3 -> 6; matrix products, arithmetic and copies ran while one was open for 0% -> 0% of each run, Pallas kernels for 0% -> 0%
where the time goes in v2:
time: 28.9 us; the launch traced here: 28.7 us
  starting transfers between devices  11.8 us (41%)
  waiting for transfers between devices  11.7 us (40%)
  Pallas kernels  3.91 us (14%)
  between operations  0.72 us (2%)
  other arithmetic  0.62 us (2%)
    ppermute x6, starting transfers between devices, exchange(): lax.ppermute(block, 'seq', [(i, i ^ 2 * k) for i in range(count)])  10.1 us
    ppermute x6, waiting for transfers between devices, exchange(): lax.ppermute(block, 'seq', [(i, i ^ 2 * k) for i in range(count)])  7.42 us
    ppermute x1, waiting for transfers between devices, by_pairs(): lax.ppermute(packed, 'seq', [(i, i ^ 1) for i in range(sequences)])  3.04 us
    pallas_call x1, Pallas kernels, by_pairs(): pl.pallas_call(functools.partial(pair_project_kernel, pairs, layers, 4 *...  2.28 us
    ppermute x1, starting transfers between devices, by_pairs(): lax.ppermute(packed, 'seq', [(i, i ^ 1) for i in range(sequences)])  1.56 us
    ppermute x1, waiting for transfers between devices, by_pairs(): arrived = lax.ppermute(other, 'head', [(0, 1), (1, 0)])  1.19 us
    pallas_call x1, Pallas kernels, by_pairs(): pl.pallas_call(functools.partial(stage_kernel, pairs), out_shape=[block_s...  0.85 us
    pallas_call x1, Pallas kernels, by_pairs(): pl.pallas_call(functools.partial(pair_attend_kernel, pairs, layers, kv_he...  0.77 us
  transfers between devices with their start and end apart: 8, of which 6 were waited for; matrix products, arithmetic and copies ran while one was open for 0% of the time, Pallas kernels for 0%

profile of v2, /device:TPU:0, one launch (start us, length us, event | category | flops | bytes accessed | tf_op | source)
XLA Modules:
  0.0 28.7 jit_solution(2788698795073958897)
XLA Ops:
  0.7 0.9 %shard_map.82 = (bf16[2,2,16,128]{3,2,1,0:T(8,128)(2,1)S(1)}, bf16[2,2,16,128]{3,2,1,0:T(8,128)(2,1)S(1)}, bf16[2,2,16,128]{3,2,1,0:T(8,128)(2,1)S(1)}, bf16[2,2...) custom-call(s32[1]{0:T(128)S(6)} %copy.9.len_ref, s32[8]{0:T(128)} %slot_hbm.1, bf16[2,8,8,128]{3,2,1,0:T(8,128)(2,1)} %bitcast.7, ...), custom_call_target="tpu_custom_call" | custom-call | flops 10000000000 | bytes 1048576 | tf_op jit(solution)/shard_map/pallas_call | solution.py:337
  1.5 3.1 %collective-permute-start = (bf16[2,2,16,128]{3,2,1,0:T(8,128)(2,1)S(1)}, bf16[2,2,16,128]{3,2,1,0:T(8,128)(2,1)S(1)}, u32[]{:S(2)}, u32[]{:S(2)}) collective-permute-start(bf16[2,2,16,128]{3,2,1,0:T(8,128)(2,1)S(1)} %get-tuple-element.13), channel_id=1, source_target_pairs={{0,4},{2,6},{4,0},{6,2},{8,12},{10,14},{12,8},{14,10},{1,5},{3,7},... | collective-permute-start | bytes 49160 | tf_op jit(solution)/shard_map/ppermute | solution.py:302
  4.6 2.6 %collective-permute-start.1 = (bf16[2,2,16,128]{3,2,1,0:T(8,128)(2,1)S(1)}, bf16[2,2,16,128]{3,2,1,0:T(8,128)(2,1)S(1)}, u32[]{:S(2)}, u32[]{:S(2)}) collective-permute-start(bf16[2,2,16,128]{3,2,1,0:T(8,128)(2,1)S(1)} %get-tuple-element.14), channel_id=1, source_target_pairs={{0,8},{2,10},{4,12},{6,14},{8,0},{10,2},{12,4},{14,6},{1,9},{3,11}... | collective-permute-start | bytes 49160 | tf_op jit(solution)/shard_map/ppermute | solution.py:302
  7.2 0.0 collective-permute-start.2
  7.2 0.0 collective-permute-done.refs_1_
  7.2 2.1 %collective-permute-done.1.refs_2_ = bf16[2,2,16,128]{3,2,1,0:T(8,128)(2,1)S(1)} collective-permute-done((bf16[2,2,16,128]{3,2,1,0:T(8,128)(2,1)S(1)}, bf16[2,2,16,128]{3,2,1,0:T(8,128)(2,1)S(1)}, u32[]{:S(2)}, u32[]{:S(2)}) %collective-permute-start.1) | collective-permute-done | bytes 16416 | tf_op jit(solution)/shard_map/ppermute | solution.py:302
  9.3 3.4 %collective-permute-done.2.refs_3_ = bf16[2,2,16,128]{3,2,1,0:T(8,128)(2,1)S(1)} collective-permute-done((bf16[2,2,16,128]{3,2,1,0:T(8,128)(2,1)S(1)}, bf16[2,2,16,128]{3,2,1,0:T(8,128)(2,1)S(1)}, u32[]{:S(2)}, u32[]{:S(2)}) %collective-permute-start.2) | collective-permute-done | bytes 16416 | tf_op jit(solution)/shard_map/ppermute | solution.py:302
  12.8 0.0 slice-start.2
  12.8 0.0 slice-start.3
  12.8 1.6 %collective-permute-start.3 = (bf16[352,128]{1,0:T(8,128)(2,1)S(1)}, bf16[352,128]{1,0:T(8,128)(2,1)S(1)}, u32[]{:S(2)}, u32[]{:S(2)}) collective-permute-start(bf16[352,128]{1,0:T(8,128)(2,1)S(1)} %shard_map.83), channel_id=1, source_target_pairs={{0,2},{2,0},{4,6},{6,4},{8,10},{10,8},{12,14},{14,12},{1,3},{3,1},... | collective-permute-start | bytes 270344 | tf_op jit(solution)/shard_map/ppermute | solution.py:370
  14.4 3.0 %collective-permute-done.3.refs_5_ = bf16[352,128]{1,0:T(8,128)(2,1)S(1)} collective-permute-done((bf16[352,128]{1,0:T(8,128)(2,1)S(1)}, bf16[352,128]{1,0:T(8,128)(2,1)S(1)}, u32[]{:S(2)}, u32[]{:S(2)}) %collective-permute-start.3) | collective-permute-done | bytes 90144 | tf_op jit(solution)/shard_map/ppermute | solution.py:370
  17.4 0.8 %shard_map.84.refs_0_ = bf16[2,64,128]{2,1,0:T(8,128)(2,1)S(1)} custom-call(bf16[2,2,16,128]{3,2,1,0:T(8,128)(2,1)S(1)} %get-tuple-element.12.refs_0_, bf16[2,2,16,128]{3,2,1,0:T(8,128)(2,1)S(1)} %collective-permute-done.refs_1_, bf16[2,2,16,128]{3,2,1,0:T(8,128)(2,1)S(1)} %collective-permute-done.1.refs_2_, ...), custom_call_target="tpu_custom_call" | custom-call | flops 10000000000 | bytes 1048576 | tf_op jit(solution)/shard_map/pallas_call | solution.py:371
  18.2 0.2 collective-permute-start.6
  18.4 0.0 collective-permute-start.5
  18.4 4.2 %collective-permute-start.4 = (bf16[2,64,128]{2,1,0:T(8,128)(2,1)S(1)}, bf16[2,64,128]{2,1,0:T(8,128)(2,1)S(1)}, u32[]{:S(2)}, u32[]{:S(2)}) collective-permute-start(bf16[2,64,128]{2,1,0:T(8,128)(2,1)S(1)} %shard_map.84.refs_0_), channel_id=1, source_target_pairs={{0,4},{2,6},{4,0},{6,2},{8,12},{10,14},{12,8},{14,10},{1,5},{3,7},... | collective-permute-start | bytes 98312 | tf_op jit(solution)/shard_map/ppermute | solution.py:302
  22.6 1.3 %collective-permute-done.6.refs_3_ = bf16[2,64,128]{2,1,0:T(8,128)(2,1)S(1)} collective-permute-done((bf16[2,64,128]{2,1,0:T(8,128)(2,1)S(1)}, bf16[2,64,128]{2,1,0:T(8,128)(2,1)S(1)}, u32[]{:S(2)}, u32[]{:S(2)}) %collective-permute-start.6) | collective-permute-done | bytes 32800 | tf_op jit(solution)/shard_map/ppermute | solution.py:302
  23.9 0.0 collective-permute-done.5.refs_2_
  23.9 0.6 %collective-permute-done.4.refs_1_ = bf16[2,64,128]{2,1,0:T(8,128)(2,1)S(1)} collective-permute-done((bf16[2,64,128]{2,1,0:T(8,128)(2,1)S(1)}, bf16[2,64,128]{2,1,0:T(8,128)(2,1)S(1)}, u32[]{:S(2)}, u32[]{:S(2)}) %collective-permute-start.4) | collective-permute-done | bytes 32800 | tf_op jit(solution)/shard_map/ppermute | solution.py:302
  24.5 0.0 slice-done.2
  24.5 0.0 slice-done.3
  24.5 2.3 %shard_map.85 = (f32[2,4,1024]{2,1,0:T(4,128)S(1)}, f32[2,4,1024]{2,1,0:T(4,128)S(1)}) custom-call(bf16[2,64,128]{2,1,0:T(8,128)(2,1)S(1)} %shard_map.84.refs_0_, bf16[2,64,128]{2,1,0:T(8,128)(2,1)S(1)} %collective-permute-done.4.refs_1_, bf16[2,64,128]{2,1,0:T(8,128)(2,1)S(1)} %collective-permute-done.5.refs_2_, ...), custom_call_target="tpu_custom_call" | custom-call | tf_op jit(solution)/shard_map/pallas_call | solution.py:381
  26.8 0.1 collective-permute-start.7
  26.9 1.2 %collective-permute-done.7 = f32[2,4,1024]{2,1,0:T(4,128)S(1)} collective-permute-done((f32[2,4,1024]{2,1,0:T(4,128)S(1)}, f32[2,4,1024]{2,1,0:T(4,128)S(1)}, u32[]{:S(2)}, u32[]{:S(2)}) %collective-permute-start.7) | collective-permute-done | bytes 32800 | tf_op jit(solution)/shard_map/ppermute | solution.py:389
  28.1 0.6 %add_convert_fusion = bf16[2,4,1024]{2,1,0:T(4,128)(2,1)} fusion(f32[2,4,1024]{2,1,0:T(4,128)S(1)} %get-tuple-element.17, f32[2,4,1024]{2,1,0:T(4,128)S(1)} %collective-permute-done.7), kind=kLoop, calls=%fused_computation | loop fusion | flops 16384 | bytes 81920 | tf_op jit(solution)/shard_map/convert_element_type | solution.py:390
  (6 shorter events, 0.0 us)
Async XLA Ops:
  1.5 5.7 %collective-permute-start = (bf16[2,2,16,128]{3,2,1,0:T(8,128)(2,1)S(1)}, bf16[2,2,16,128]{3,2,1,0:T(8,128)(2,1)S(1)}, u32[]{:S(2)}, u32[]{:S(2)}) collective-permute-start(bf16[2,2,16,128]{3,2,1,0:T(8,128)(2,1)S(1)} %get-tuple-element.13), channel_id=1, source_target_pairs={{0,4},{2,6},{4,0},{6,2},{8,12},{10,14},{12,8},{14,10},{1,5},{3,7},... | collective-permute-start | bytes 49160 | tf_op jit(solution)/shard_map/ppermute | solution.py:302
  4.6 4.7 %collective-permute-start.1 = (bf16[2,2,16,128]{3,2,1,0:T(8,128)(2,1)S(1)}, bf16[2,2,16,128]{3,2,1,0:T(8,128)(2,1)S(1)}, u32[]{:S(2)}, u32[]{:S(2)}) collective-permute-start(bf16[2,2,16,128]{3,2,1,0:T(8,128)(2,1)S(1)} %get-tuple-element.14), channel_id=1, source_target_pairs={{0,8},{2,10},{4,12},{6,14},{8,0},{10,2},{12,4},{14,6},{1,9},{3,11}... | collective-permute-start | bytes 49160 | tf_op jit(solution)/shard_map/ppermute | solution.py:302
  7.2 5.5 %collective-permute-start.2 = (bf16[2,2,16,128]{3,2,1,0:T(8,128)(2,1)S(1)}, bf16[2,2,16,128]{3,2,1,0:T(8,128)(2,1)S(1)}, u32[]{:S(2)}, u32[]{:S(2)}) collective-permute-start(bf16[2,2,16,128]{3,2,1,0:T(8,128)(2,1)S(1)} %get-tuple-element.15), channel_id=1, source_target_pairs={{0,12},{2,14},{4,8},{6,10},{8,4},{10,6},{12,0},{14,2},{1,13},{3,15... | collective-permute-start | bytes 49160 | tf_op jit(solution)/shard_map/ppermute | solution.py:302
  12.8 11.7 %slice-start = ((s8[16777216]{0:T(1024)(128)(4,1)}), s8[4194304]{0:T(1024)(128)(4,1)S(1)}, s32[]{:S(2)}) async-start(s8[16777216]{0:T(1024)(128)(4,1)} %bitcast.5), calls=%async_computation | async-start | bytes 8388608
  12.8 11.7 %slice-start.1 = ((s8[16777216]{0:T(1024)(128)(4,1)}), s8[4194304]{0:T(1024)(128)(4,1)S(1)}, s32[]{:S(2)}) async-start(s8[16777216]{0:T(1024)(128)(4,1)} %bitcast.5), calls=%async_computation.1 | async-start | bytes 8388608
  12.8 11.7 %slice-start.2 = ((s8[16777216]{0:T(1024)(128)(4,1)}), s8[4194304]{0:T(1024)(128)(4,1)S(1)}, s32[]{:S(2)}) async-start(s8[16777216]{0:T(1024)(128)(4,1)} %bitcast.5), calls=%async_computation.2 | async-start | bytes 8388608
  12.8 11.7 %slice-start.3 = ((s8[16777216]{0:T(1024)(128)(4,1)}), s8[4194304]{0:T(1024)(128)(4,1)S(1)}, s32[]{:S(2)}) async-start(s8[16777216]{0:T(1024)(128)(4,1)} %bitcast.5), calls=%async_computation.3 | async-start | bytes 8388608
  12.8 4.6 %collective-permute-start.3 = (bf16[352,128]{1,0:T(8,128)(2,1)S(1)}, bf16[352,128]{1,0:T(8,128)(2,1)S(1)}, u32[]{:S(2)}, u32[]{:S(2)}) collective-permute-start(bf16[352,128]{1,0:T(8,128)(2,1)S(1)} %shard_map.83), channel_id=1, source_target_pairs={{0,2},{2,0},{4,6},{6,4},{8,10},{10,8},{12,14},{14,12},{1,3},{3,1},... | collective-permute-start | bytes 270344 | tf_op jit(solution)/shard_map/ppermute | solution.py:370
  18.2 5.8 %collective-permute-start.6 = (bf16[2,64,128]{2,1,0:T(8,128)(2,1)S(1)}, bf16[2,64,128]{2,1,0:T(8,128)(2,1)S(1)}, u32[]{:S(2)}, u32[]{:S(2)}) collective-permute-start(bf16[2,64,128]{2,1,0:T(8,128)(2,1)S(1)} %shard_map.84.refs_0_), channel_id=1, source_target_pairs={{0,12},{2,14},{4,8},{6,10},{8,4},{10,6},{12,0},{14,2},{1,13},{3,15... | collective-permute-start | bytes 98312 | tf_op jit(solution)/shard_map/ppermute | solution.py:302
  18.4 5.5 %collective-permute-start.5 = (bf16[2,64,128]{2,1,0:T(8,128)(2,1)S(1)}, bf16[2,64,128]{2,1,0:T(8,128)(2,1)S(1)}, u32[]{:S(2)}, u32[]{:S(2)}) collective-permute-start(bf16[2,64,128]{2,1,0:T(8,128)(2,1)S(1)} %shard_map.84.refs_0_), channel_id=1, source_target_pairs={{0,8},{2,10},{4,12},{6,14},{8,0},{10,2},{12,4},{14,6},{1,9},{3,11}... | collective-permute-start | bytes 98312 | tf_op jit(solution)/shard_map/ppermute | solution.py:302
  18.4 6.1 %collective-permute-start.4 = (bf16[2,64,128]{2,1,0:T(8,128)(2,1)S(1)}, bf16[2,64,128]{2,1,0:T(8,128)(2,1)S(1)}, u32[]{:S(2)}, u32[]{:S(2)}) collective-permute-start(bf16[2,64,128]{2,1,0:T(8,128)(2,1)S(1)} %shard_map.84.refs_0_), channel_id=1, source_target_pairs={{0,4},{2,6},{4,0},{6,2},{8,12},{10,14},{12,8},{14,10},{1,5},{3,7},... | collective-permute-start | bytes 98312 | tf_op jit(solution)/shard_map/ppermute | solution.py:302
  26.8 1.3 %collective-permute-start.7 = (f32[2,4,1024]{2,1,0:T(4,128)S(1)}, f32[2,4,1024]{2,1,0:T(4,128)S(1)}, u32[]{:S(2)}, u32[]{:S(2)}) collective-permute-start(f32[2,4,1024]{2,1,0:T(4,128)S(1)} %get-tuple-element.18), channel_id=1, source_target_pairs={{0,1},{1,0},{2,3},{3,2},{4,5},{5,4},{6,7},{7,6},{8,9},{9,8},{10,11... | collective-permute-start | bytes 98312 | tf_op jit(solution)/shard_map/ppermute | solution.py:389

commit v3 on v2

--- a/solution.py
+++ b/solution.py
@@ -6,6 +6,7 @@
 from jax.experimental import pallas as pl
 from jax.experimental.pallas import tpu as pltpu
 from jax.sharding import PartitionSpec as P
+
 
 VMEM = pl.BlockSpec(memory_space=pltpu.VMEM)
 SMEM = pl.BlockSpec(memory_space=pltpu.SMEM)
@@ -150,7 +151,6 @@
 
 def stage_kernel(
     pairs,
-    len_ref,
     slot_hbm,
     keys_hbm,
     values_hbm,
@@ -180,11 +180,6 @@
         copy.start()
     for copy in copies:
         copy.wait()
-    tail = query_rows + 2 * new_rows
-    length = len_ref[0].astype(jnp.float32)
-    side_ref[tail:, :] = jnp.full((side_ref.shape[0] - tail, side_ref.shape[1]), length).astype(
-        jnp.bfloat16
-    )
     pair, _ = place()
     for k in range(pairs):
         for side in range(2):
@@ -203,9 +198,9 @@
 
 
 def pair_attend_kernel(pairs, layers, kv_heads, query_rows, *refs):
-    blocks, side_ref, partner_ref, out_ref = refs[:pairs], refs[pairs], refs[pairs + 1], refs[-1]
+    blocks, (side_ref, limit_ref, partner_ref, out_ref) = refs[:pairs], refs[pairs:]
     pair, mine = place()
-    _, _, block, depth = blocks[0].shape
+    _, _, block, _ = blocks[0].shape
     groups = layers * kv_heads
     positions = block // groups
     per_block = 4 * block
@@ -243,8 +238,11 @@
         queries = side_rows(sequence, 0, query_rows)
         new_keys = side_rows(sequence, query_rows, groups)
         new_values = side_rows(sequence, query_rows + groups, groups)
-        length = side_rows(sequence, query_rows + 2 * groups, 16)[:1, :1].astype(jnp.float32)
-        allowed = same_group & (position.astype(jnp.float32) < length[None])
+        limit = jnp.where(
+            mine == sequence, limit_ref[...], partner_ref[tail + query_rows + 2 * groups :, :]
+        )
+        limit = limit[:1, :1].astype(jnp.float32)
+        allowed = same_group & (position.astype(jnp.float32) < limit[None])
         out_ref[sequence] = softmax_context(
             queries, new_keys, new_values, stacked[0], stacked[1], allowed, groups
         )
@@ -298,11 +296,11 @@
 
 def exchange(blocks):
     count = 2 * len(blocks)
-    return [blocks[0]] + [
-        lax.ppermute(block, "seq", [(i, i ^ (2 * k)) for i in range(count)])
-        for k, block in enumerate(blocks)
-        if k
-    ]
+    arrived = [blocks[0]]
+    for k in range(1, len(blocks)):
+        pairs = [(i, i ^ (2 * k)) for i in range(count)]
+        arrived.append(lax.ppermute(blocks[k], "seq", pairs))
+    return arrived
 
 
 def params(limit):
@@ -332,12 +330,12 @@
     flat = (layers, sequences, positions * kv_heads, depth)
     block = layers * positions * kv_heads
     query_rows, groups = layers * heads, layers * kv_heads
-    side_rows = query_rows + 2 * groups + 16
+    side_rows = query_rows + 2 * groups
     block_shape = jax.ShapeDtypeStruct((2, 2, block, depth), bf16)
     *blocks, side = pl.pallas_call(
         functools.partial(stage_kernel, pairs),
         out_shape=[block_shape] * pairs + [jax.ShapeDtypeStruct((side_rows, depth), bf16)],
-        in_specs=[SMEM] + [HBM] * 6,
+        in_specs=[HBM] * 6,
         out_specs=[VMEM] * (pairs + 1),
         scratch_shapes=[
             pltpu.SMEM((sequences,), jnp.int32),
@@ -348,7 +346,6 @@
         compiler_params=params(4),
         cost_estimate=COVER,
     )(
-        lengths,
         *in_hbm(
             slot_index,
             cache_keys.reshape(flat),
@@ -359,23 +356,24 @@
         ),
     )
     blocks = exchange(blocks)
+    limit = jnp.broadcast_to(lengths.astype(bf16)[:, None], (16, depth))
     packed = pl.pallas_call(
         pack_kernel,
-        out_shape=jax.ShapeDtypeStruct((pairs * 4 * block + side_rows, depth), bf16),
-        in_specs=[VMEM] * (pairs + 1),
+        out_shape=jax.ShapeDtypeStruct((pairs * 4 * block + side_rows + 16, depth), bf16),
+        in_specs=[VMEM] * (pairs + 2),
         out_specs=VMEM,
         compiler_params=params(4),
         cost_estimate=COVER,
-    )(*blocks, side)
+    )(*blocks, side, limit)
     partner = lax.ppermute(packed, "seq", [(i, i ^ 1) for i in range(sequences)])
     contexts = pl.pallas_call(
         functools.partial(pair_attend_kernel, pairs, layers, kv_heads, query_rows),
         out_shape=jax.ShapeDtypeStruct((2, query_rows, depth), bf16),
-        in_specs=[VMEM] * (pairs + 2),
+        in_specs=[VMEM] * (pairs + 3),
         out_specs=VMEM,
         compiler_params=params(4),
         cost_estimate=COVER,
-    )(*blocks, side, partner)
+    )(*blocks, side, limit, partner)
     contexts = exchange([contexts] * pairs)
     part = jax.ShapeDtypeStruct((layers, sequences // 2, columns), f32)
     mine, other = pl.pallas_call(
@@ -462,10 +460,15 @@
     )
     seq = mesh.shape["seq"]
     few = seq in (2, 4, 8)
-    return jax.shard_map(
-        by_pairs if few else by_all_to_all,
+
+    def step(*operands):
+        return (by_pairs if few else by_all_to_all)(*operands)
+
+    step = jax.shard_map(
+        step,
         mesh=mesh,
         in_specs=placed,
         out_specs=P(None, ("grp", "head"), "seq"),
         check_vma=False,
     )
+    return step

time: 28.9 us -> 28.2 us (0.976)
  waiting for transfers between devices: 11.7 us -> 11 us
    ppermute x6, waiting for transfers between devices: 7.42 us -> 6.76 us  [exchange(): arrived.append(lax.ppermute(blocks[k], 'seq', pairs))]
where the time goes in v3:
time: 28.2 us; the launch traced here: 28 us
  starting transfers between devices  11.8 us (42%)
  waiting for transfers between devices  11 us (39%)
  Pallas kernels  3.9 us (14%)
  between operations  0.73 us (3%)
  other arithmetic  0.62 us (2%)
    ppermute x6, starting transfers between devices, exchange(): arrived.append(lax.ppermute(blocks[k], 'seq', pairs))  10.1 us
    ppermute x6, waiting for transfers between devices, exchange(): arrived.append(lax.ppermute(blocks[k], 'seq', pairs))  6.76 us
    ppermute x1, waiting for transfers between devices, by_pairs(): lax.ppermute(packed, 'seq', [(i, i ^ 1) for i in range(sequences)])  3.04 us
    pallas_call x1, Pallas kernels, by_pairs(): pl.pallas_call(functools.partial(pair_project_kernel, pairs, layers, 4 *...  2.28 us
    ppermute x1, starting transfers between devices, by_pairs(): lax.ppermute(packed, 'seq', [(i, i ^ 1) for i in range(sequences)])  1.56 us
    ppermute x1, waiting for transfers between devices, by_pairs(): arrived = lax.ppermute(other, 'head', [(0, 1), (1, 0)])  1.19 us
    pallas_call x1, Pallas kernels, by_pairs(): pl.pallas_call(functools.partial(stage_kernel, pairs), out_shape=[block_s...  0.85 us
    pallas_call x1, Pallas kernels, by_pairs(): pl.pallas_call(functools.partial(pair_attend_kernel, pairs, layers, kv_he...  0.77 us
  transfers between devices with their start and end apart: 8, of which 6 were waited for; matrix products, arithmetic and copies ran while one was open for 0% of the time, Pallas kernels for 0%

profile of v3, /device:TPU:0, one launch (start us, length us, event | category | flops | bytes accessed | tf_op | source)
XLA Modules:
  0.0 28.0 jit_solution(14091509774727464404)
XLA Ops:
  0.0 0.8 %shard_map.82 = (bf16[2,2,16,128]{3,2,1,0:T(8,128)(2,1)S(1)}, bf16[2,2,16,128]{3,2,1,0:T(8,128)(2,1)S(1)}, bf16[2,2,16,128]{3,2,1,0:T(8,128)(2,1)S(1)}, bf16[2,2...) custom-call(s32[8]{0:T(128)} %slot_hbm.1, bf16[2,8,8,128]{3,2,1,0:T(8,128)(2,1)} %bitcast.8, ...), custom_call_target="tpu_custom_call" | custom-call | flops 10000000000 | bytes 1048576 | tf_op jit(solution)/shard_map/pallas_call | solution.py:335
  0.9 3.1 %collective-permute-start = (bf16[2,2,16,128]{3,2,1,0:T(8,128)(2,1)S(1)}, bf16[2,2,16,128]{3,2,1,0:T(8,128)(2,1)S(1)}, u32[]{:S(2)}, u32[]{:S(2)}) collective-permute-start(bf16[2,2,16,128]{3,2,1,0:T(8,128)(2,1)S(1)} %get-tuple-element.13), channel_id=1, source_target_pairs={{0,4},{2,6},{4,0},{6,2},{8,12},{10,14},{12,8},{14,10},{1,5},{3,7},... | collective-permute-start | bytes 49160 | tf_op jit(solution)/shard_map/ppermute | solution.py:302
  4.0 2.6 %collective-permute-start.1 = (bf16[2,2,16,128]{3,2,1,0:T(8,128)(2,1)S(1)}, bf16[2,2,16,128]{3,2,1,0:T(8,128)(2,1)S(1)}, u32[]{:S(2)}, u32[]{:S(2)}) collective-permute-start(bf16[2,2,16,128]{3,2,1,0:T(8,128)(2,1)S(1)} %get-tuple-element.14), channel_id=1, source_target_pairs={{0,8},{2,10},{4,12},{6,14},{8,0},{10,2},{12,4},{14,6},{1,9},{3,11}... | collective-permute-start | bytes 49160 | tf_op jit(solution)/shard_map/ppermute | solution.py:302
  6.6 0.0 collective-permute-start.2
  7.2 0.0 collective-permute-done.refs_1_
  7.2 1.5 %collective-permute-done.1.refs_2_ = bf16[2,2,16,128]{3,2,1,0:T(8,128)(2,1)S(1)} collective-permute-done((bf16[2,2,16,128]{3,2,1,0:T(8,128)(2,1)S(1)}, bf16[2,2,16,128]{3,2,1,0:T(8,128)(2,1)S(1)}, u32[]{:S(2)}, u32[]{:S(2)}) %collective-permute-start.1) | collective-permute-done | bytes 16416 | tf_op jit(solution)/shard_map/ppermute | solution.py:302
  8.7 3.4 %collective-permute-done.2.refs_3_ = bf16[2,2,16,128]{3,2,1,0:T(8,128)(2,1)S(1)} collective-permute-done((bf16[2,2,16,128]{3,2,1,0:T(8,128)(2,1)S(1)}, bf16[2,2,16,128]{3,2,1,0:T(8,128)(2,1)S(1)}, u32[]{:S(2)}, u32[]{:S(2)}) %collective-permute-start.2) | collective-permute-done | bytes 16416 | tf_op jit(solution)/shard_map/ppermute | solution.py:302
  12.1 0.0 slice-start.2
  12.1 0.0 slice-start.3
  12.1 1.6 %collective-permute-start.3 = (bf16[352,128]{1,0:T(8,128)(2,1)S(1)}, bf16[352,128]{1,0:T(8,128)(2,1)S(1)}, u32[]{:S(2)}, u32[]{:S(2)}) collective-permute-start(bf16[352,128]{1,0:T(8,128)(2,1)S(1)} %shard_map.83), channel_id=1, source_target_pairs={{0,2},{2,0},{4,6},{6,4},{8,10},{10,8},{12,14},{14,12},{1,3},{3,1},... | collective-permute-start | bytes 270344 | tf_op jit(solution)/shard_map/ppermute | solution.py:368
  13.7 3.0 %collective-permute-done.3.refs_6_ = bf16[352,128]{1,0:T(8,128)(2,1)S(1)} collective-permute-done((bf16[352,128]{1,0:T(8,128)(2,1)S(1)}, bf16[352,128]{1,0:T(8,128)(2,1)S(1)}, u32[]{:S(2)}, u32[]{:S(2)}) %collective-permute-start.3) | collective-permute-done | bytes 90144 | tf_op jit(solution)/shard_map/ppermute | solution.py:368
  16.7 0.8 %shard_map.84.refs_0_ = bf16[2,64,128]{2,1,0:T(8,128)(2,1)S(1)} custom-call(bf16[2,2,16,128]{3,2,1,0:T(8,128)(2,1)S(1)} %get-tuple-element.12.refs_0_, bf16[2,2,16,128]{3,2,1,0:T(8,128)(2,1)S(1)} %collective-permute-done.refs_1_, bf16[2,2,16,128]{3,2,1,0:T(8,128)(2,1)S(1)} %collective-permute-done.1.refs_2_, ...), custom_call_target="tpu_custom_call" | custom-call | flops 10000000000 | bytes 1048576 | tf_op jit(solution)/shard_map/pallas_call | solution.py:369
  17.5 0.2 collective-permute-start.6
  17.7 0.0 collective-permute-start.5
  17.7 4.2 %collective-permute-start.4 = (bf16[2,64,128]{2,1,0:T(8,128)(2,1)S(1)}, bf16[2,64,128]{2,1,0:T(8,128)(2,1)S(1)}, u32[]{:S(2)}, u32[]{:S(2)}) collective-permute-start(bf16[2,64,128]{2,1,0:T(8,128)(2,1)S(1)} %shard_map.84.refs_0_), channel_id=1, source_target_pairs={{0,4},{2,6},{4,0},{6,2},{8,12},{10,14},{12,8},{14,10},{1,5},{3,7},... | collective-permute-start | bytes 98312 | tf_op jit(solution)/shard_map/ppermute | solution.py:302
  21.9 1.3 %collective-permute-done.6.refs_3_ = bf16[2,64,128]{2,1,0:T(8,128)(2,1)S(1)} collective-permute-done((bf16[2,64,128]{2,1,0:T(8,128)(2,1)S(1)}, bf16[2,64,128]{2,1,0:T(8,128)(2,1)S(1)}, u32[]{:S(2)}, u32[]{:S(2)}) %collective-permute-start.6) | collective-permute-done | bytes 32800 | tf_op jit(solution)/shard_map/ppermute | solution.py:302
  23.3 0.0 collective-permute-done.5.refs_2_
  23.3 0.6 %collective-permute-done.4.refs_1_ = bf16[2,64,128]{2,1,0:T(8,128)(2,1)S(1)} collective-permute-done((bf16[2,64,128]{2,1,0:T(8,128)(2,1)S(1)}, bf16[2,64,128]{2,1,0:T(8,128)(2,1)S(1)}, u32[]{:S(2)}, u32[]{:S(2)}) %collective-permute-start.4) | collective-permute-done | bytes 32800 | tf_op jit(solution)/shard_map/ppermute | solution.py:302
  23.8 0.0 slice-done
  23.8 0.0 slice-done.2
  23.9 2.3 %shard_map.85 = (f32[2,4,1024]{2,1,0:T(4,128)S(1)}, f32[2,4,1024]{2,1,0:T(4,128)S(1)}) custom-call(bf16[2,64,128]{2,1,0:T(8,128)(2,1)S(1)} %shard_map.84.refs_0_, bf16[2,64,128]{2,1,0:T(8,128)(2,1)S(1)} %collective-permute-done.4.refs_1_, bf16[2,64,128]{2,1,0:T(8,128)(2,1)S(1)} %collective-permute-done.5.refs_2_, ...), custom_call_target="tpu_custom_call" | custom-call | tf_op jit(solution)/shard_map/pallas_call | solution.py:379
  26.1 0.1 collective-permute-start.7
  26.2 1.2 %collective-permute-done.7 = f32[2,4,1024]{2,1,0:T(4,128)S(1)} collective-permute-done((f32[2,4,1024]{2,1,0:T(4,128)S(1)}, f32[2,4,1024]{2,1,0:T(4,128)S(1)}, u32[]{:S(2)}, u32[]{:S(2)}) %collective-permute-start.7) | collective-permute-done | bytes 32800 | tf_op jit(solution)/shard_map/ppermute | solution.py:387
  27.4 0.6 %add_convert_fusion = bf16[2,4,1024]{2,1,0:T(4,128)(2,1)} fusion(f32[2,4,1024]{2,1,0:T(4,128)S(1)} %get-tuple-element.17, f32[2,4,1024]{2,1,0:T(4,128)S(1)} %collective-permute-done.7), kind=kLoop, calls=%fused_computation | loop fusion | flops 16384 | bytes 81920 | tf_op jit(solution)/shard_map/convert_element_type | solution.py:388
  (7 shorter events, 0.0 us)
Async XLA Ops:
  0.9 6.4 %collective-permute-start = (bf16[2,2,16,128]{3,2,1,0:T(8,128)(2,1)S(1)}, bf16[2,2,16,128]{3,2,1,0:T(8,128)(2,1)S(1)}, u32[]{:S(2)}, u32[]{:S(2)}) collective-permute-start(bf16[2,2,16,128]{3,2,1,0:T(8,128)(2,1)S(1)} %get-tuple-element.13), channel_id=1, source_target_pairs={{0,4},{2,6},{4,0},{6,2},{8,12},{10,14},{12,8},{14,10},{1,5},{3,7},... | collective-permute-start | bytes 49160 | tf_op jit(solution)/shard_map/ppermute | solution.py:302
  4.0 4.7 %collective-permute-start.1 = (bf16[2,2,16,128]{3,2,1,0:T(8,128)(2,1)S(1)}, bf16[2,2,16,128]{3,2,1,0:T(8,128)(2,1)S(1)}, u32[]{:S(2)}, u32[]{:S(2)}) collective-permute-start(bf16[2,2,16,128]{3,2,1,0:T(8,128)(2,1)S(1)} %get-tuple-element.14), channel_id=1, source_target_pairs={{0,8},{2,10},{4,12},{6,14},{8,0},{10,2},{12,4},{14,6},{1,9},{3,11}... | collective-permute-start | bytes 49160 | tf_op jit(solution)/shard_map/ppermute | solution.py:302
  6.6 5.5 %collective-permute-start.2 = (bf16[2,2,16,128]{3,2,1,0:T(8,128)(2,1)S(1)}, bf16[2,2,16,128]{3,2,1,0:T(8,128)(2,1)S(1)}, u32[]{:S(2)}, u32[]{:S(2)}) collective-permute-start(bf16[2,2,16,128]{3,2,1,0:T(8,128)(2,1)S(1)} %get-tuple-element.15), channel_id=1, source_target_pairs={{0,12},{2,14},{4,8},{6,10},{8,4},{10,6},{12,0},{14,2},{1,13},{3,15... | collective-permute-start | bytes 49160 | tf_op jit(solution)/shard_map/ppermute | solution.py:302
  12.1 11.7 %slice-start = ((s8[16777216]{0:T(1024)(128)(4,1)}), s8[4194304]{0:T(1024)(128)(4,1)S(1)}, s32[]{:S(2)}) async-start(s8[16777216]{0:T(1024)(128)(4,1)} %bitcast.6), calls=%async_computation | async-start | bytes 8388608
  12.1 11.7 %slice-start.1 = ((s8[16777216]{0:T(1024)(128)(4,1)}), s8[4194304]{0:T(1024)(128)(4,1)S(1)}, s32[]{:S(2)}) async-start(s8[16777216]{0:T(1024)(128)(4,1)} %bitcast.6), calls=%async_computation.1 | async-start | bytes 8388608
  12.1 11.7 %slice-start.2 = ((s8[16777216]{0:T(1024)(128)(4,1)}), s8[4194304]{0:T(1024)(128)(4,1)S(1)}, s32[]{:S(2)}) async-start(s8[16777216]{0:T(1024)(128)(4,1)} %bitcast.6), calls=%async_computation.2 | async-start | bytes 8388608
  12.1 11.7 %slice-start.3 = ((s8[16777216]{0:T(1024)(128)(4,1)}), s8[4194304]{0:T(1024)(128)(4,1)S(1)}, s32[]{:S(2)}) async-start(s8[16777216]{0:T(1024)(128)(4,1)} %bitcast.6), calls=%async_computation.3 | async-start | bytes 8388608
  12.1 4.6 %collective-permute-start.3 = (bf16[352,128]{1,0:T(8,128)(2,1)S(1)}, bf16[352,128]{1,0:T(8,128)(2,1)S(1)}, u32[]{:S(2)}, u32[]{:S(2)}) collective-permute-start(bf16[352,128]{1,0:T(8,128)(2,1)S(1)} %shard_map.83), channel_id=1, source_target_pairs={{0,2},{2,0},{4,6},{6,4},{8,10},{10,8},{12,14},{14,12},{1,3},{3,1},... | collective-permute-start | bytes 270344 | tf_op jit(solution)/shard_map/ppermute | solution.py:368
  17.5 5.8 %collective-permute-start.6 = (bf16[2,64,128]{2,1,0:T(8,128)(2,1)S(1)}, bf16[2,64,128]{2,1,0:T(8,128)(2,1)S(1)}, u32[]{:S(2)}, u32[]{:S(2)}) collective-permute-start(bf16[2,64,128]{2,1,0:T(8,128)(2,1)S(1)} %shard_map.84.refs_0_), channel_id=1, source_target_pairs={{0,12},{2,14},{4,8},{6,10},{8,4},{10,6},{12,0},{14,2},{1,13},{3,15... | collective-permute-start | bytes 98312 | tf_op jit(solution)/shard_map/ppermute | solution.py:302
  17.7 5.5 %collective-permute-start.5 = (bf16[2,64,128]{2,1,0:T(8,128)(2,1)S(1)}, bf16[2,64,128]{2,1,0:T(8,128)(2,1)S(1)}, u32[]{:S(2)}, u32[]{:S(2)}) collective-permute-start(bf16[2,64,128]{2,1,0:T(8,128)(2,1)S(1)} %shard_map.84.refs_0_), channel_id=1, source_target_pairs={{0,8},{2,10},{4,12},{6,14},{8,0},{10,2},{12,4},{14,6},{1,9},{3,11}... | collective-permute-start | bytes 98312 | tf_op jit(solution)/shard_map/ppermute | solution.py:302
  17.7 6.1 %collective-permute-start.4 = (bf16[2,64,128]{2,1,0:T(8,128)(2,1)S(1)}, bf16[2,64,128]{2,1,0:T(8,128)(2,1)S(1)}, u32[]{:S(2)}, u32[]{:S(2)}) collective-permute-start(bf16[2,64,128]{2,1,0:T(8,128)(2,1)S(1)} %shard_map.84.refs_0_), channel_id=1, source_target_pairs={{0,4},{2,6},{4,0},{6,2},{8,12},{10,14},{12,8},{14,10},{1,5},{3,7},... | collective-permute-start | bytes 98312 | tf_op jit(solution)/shard_map/ppermute | solution.py:302
  26.1 1.3 %collective-permute-start.7 = (f32[2,4,1024]{2,1,0:T(4,128)S(1)}, f32[2,4,1024]{2,1,0:T(4,128)S(1)}, u32[]{:S(2)}, u32[]{:S(2)}) collective-permute-start(f32[2,4,1024]{2,1,0:T(4,128)S(1)} %get-tuple-element.18), channel_id=1, source_target_pairs={{0,1},{1,0},{2,3},{3,2},{4,5},{5,4},{6,7},{7,6},{8,9},{9,8},{10,11... | collective-permute-start | bytes 98312 | tf_op jit(solution)/shard_map/ppermute | solution.py:387

commit v4 on v3

--- a/solution.py
+++ b/solution.py
@@ -144,9 +144,9 @@
     return context.astype(jnp.bfloat16).reshape(rows, depth)
 
 
-def place():
+def place(pairs):
     index = lax.axis_index("seq")
-    return index // 2, index % 2
+    return index % pairs, index // pairs
 
 
 def stage_kernel(
@@ -180,10 +180,10 @@
         copy.start()
     for copy in copies:
         copy.wait()
-    pair, _ = place()
+    pair, _ = place(pairs)
     for k in range(pairs):
         for side in range(2):
-            slot = slots[(pair ^ k) * 2 + side]
+            slot = slots[side * pairs + (pair ^ k)]
             for which, held in enumerate((keys, values)):
                 for layer in range(layers):
                     blocks[k][side, which, layer * rows : (layer + 1) * rows, :] = held[layer, slot]
@@ -199,7 +199,7 @@
 
 def pair_attend_kernel(pairs, layers, kv_heads, query_rows, *refs):
     blocks, (side_ref, limit_ref, partner_ref, out_ref) = refs[:pairs], refs[pairs:]
-    pair, mine = place()
+    pair, mine = place(pairs)
     _, _, block, _ = blocks[0].shape
     groups = layers * kv_heads
     positions = block // groups
@@ -211,7 +211,7 @@
     within = column % block
     column_group = (within // (positions * kv_heads)) * kv_heads + within % kv_heads
     source = column // block
-    source = ((source % pairs) ^ pair) * 2 + ((source // pairs) ^ mine)
+    source = ((source // pairs) ^ mine) * pairs + ((source % pairs) ^ pair)
     position = source * positions + (within // kv_heads) % positions
     same_group = column_group == group
     tail = pairs * per_block
@@ -254,13 +254,15 @@
     heads = rows // layers
     sequences = 2 * pairs
     columns = weight_ref.shape[2]
+    pair, _ = place(pairs)
     for k in range(pairs):
-        wide[k * 2 * rows : (k + 1) * 2 * rows, :] = (
-            contexts[k][...].astype(jnp.float32).reshape(2 * rows, depth)
-        )
+        for side in range(2):
+            sequence = side * pairs + (pair ^ k)
+            wide[pl.ds(pl.multiple_of(sequence * rows, rows), rows), :] = contexts[k][side].astype(
+                jnp.float32
+            )
     heads_per_chunk = chunk // depth
     half = sequences // 2
-    pair, _ = place()
     first = lax.axis_index("head") == 0
     for layer in range(layers):
         total = jnp.zeros((sequences, columns), jnp.float32)
@@ -277,18 +279,6 @@
                 weight_ref[layer, c * chunk : (c + 1) * chunk, :],
                 preferred_element_type=jnp.float32,
             )
-        bit = 1
-        while bit < pairs:
-            span = 2 * bit
-            swapped = jnp.concatenate(
-                [
-                    total[(j ^ 1) * span : (j ^ 1) * span + span]
-                    for j in range(sequences // span)
-                ],
-                axis=0,
-            )
-            total = jnp.where((pair & bit) != 0, swapped, total)
-            bit *= 2
         low, high = total[:half], total[half:]
         mine_ref[layer] = jnp.where(first, low, high)
         other_ref[layer] = jnp.where(first, high, low)
@@ -298,8 +288,7 @@
     count = 2 * len(blocks)
     arrived = [blocks[0]]
     for k in range(1, len(blocks)):
-        pairs = [(i, i ^ (2 * k)) for i in range(count)]
-        arrived.append(lax.ppermute(blocks[k], "seq", pairs))
+        arrived.append(lax.ppermute(blocks[k], "seq", [(i, i ^ k) for i in range(count)]))
     return arrived
 
 
@@ -365,7 +354,7 @@
         compiler_params=params(4),
         cost_estimate=COVER,
     )(*blocks, side, limit)
-    partner = lax.ppermute(packed, "seq", [(i, i ^ 1) for i in range(sequences)])
+    partner = lax.ppermute(packed, "seq", [(i, i ^ pairs) for i in range(sequences)])
     contexts = pl.pallas_call(
         functools.partial(pair_attend_kernel, pairs, layers, kv_heads, query_rows),
         out_shape=jax.ShapeDtypeStruct((2, query_rows, depth), bf16),

time: 28.2 us -> 27.3 us (0.968)
  starting transfers between devices: 11.8 us -> 11 us
    ppermute x7, starting transfers between devices: 11.7 us -> 11 us  [the longest x6 8.13 us: exchange(): lax.ppermute(blocks[k], 'seq', [(i, i ^ k) for i in range(count)])]
where the time goes in v4:
time: 27.3 us; the launch traced here: 27.1 us
  starting transfers between devices  11 us (40%)
  waiting for transfers between devices  10.9 us (40%)
  Pallas kernels  3.9 us (14%)
  between operations  0.73 us (3%)
  other arithmetic  0.62 us (2%)
    ppermute x6, starting transfers between devices, exchange(): lax.ppermute(blocks[k], 'seq', [(i, i ^ k) for i in range(count)])  8.13 us
    ppermute x6, waiting for transfers between devices, exchange(): lax.ppermute(blocks[k], 'seq', [(i, i ^ k) for i in range(count)])  6.15 us
    ppermute x1, waiting for transfers between devices, by_pairs(): lax.ppermute(packed, 'seq', [(i, i ^ pairs) for i in range(sequences)])  3.52 us
    ppermute x1, starting transfers between devices, by_pairs(): lax.ppermute(packed, 'seq', [(i, i ^ pairs) for i in range(sequences)])  2.82 us
    pallas_call x1, Pallas kernels, by_pairs(): pl.pallas_call(functools.partial(pair_project_kernel, pairs, layers, 4 *...  2.27 us
    ppermute x1, waiting for transfers between devices, by_pairs(): arrived = lax.ppermute(other, 'head', [(0, 1), (1, 0)])  1.22 us
    pallas_call x1, Pallas kernels, by_pairs(): pl.pallas_call(functools.partial(stage_kernel, pairs), out_shape=[block_s...  0.85 us
    pallas_call x1, Pallas kernels, by_pairs(): pl.pallas_call(functools.partial(pair_attend_kernel, pairs, layers, kv_he...  0.77 us
  transfers between devices with their start and end apart: 8, of which 6 were waited for; matrix products, arithmetic and copies ran while one was open for 0% of the time, Pallas kernels for 0%

profile of v4, /device:TPU:0, one launch (start us, length us, event | category | flops | bytes accessed | tf_op | source)
XLA Modules:
  0.0 27.1 jit_solution(1510054012717033899)
XLA Ops:
  0.0 0.8 %shard_map.82 = (bf16[2,2,16,128]{3,2,1,0:T(8,128)(2,1)S(1)}, bf16[2,2,16,128]{3,2,1,0:T(8,128)(2,1)S(1)}, bf16[2,2,16,128]{3,2,1,0:T(8,128)(2,1)S(1)}, bf16[2,2...) custom-call(s32[8]{0:T(128)} %slot_hbm.1, bf16[2,8,8,128]{3,2,1,0:T(8,128)(2,1)} %bitcast.8, ...), custom_call_target="tpu_custom_call" | custom-call | flops 10000000000 | bytes 1048576 | tf_op jit(solution)/shard_map/pallas_call | solution.py:324
  0.9 3.0 %collective-permute-start = (bf16[2,2,16,128]{3,2,1,0:T(8,128)(2,1)S(1)}, bf16[2,2,16,128]{3,2,1,0:T(8,128)(2,1)S(1)}, u32[]{:S(2)}, u32[]{:S(2)}) collective-permute-start(bf16[2,2,16,128]{3,2,1,0:T(8,128)(2,1)S(1)} %get-tuple-element.13), channel_id=1, source_target_pairs={{0,2},{2,0},{4,6},{6,4},{8,10},{10,8},{12,14},{14,12},{1,3},{3,1},... | collective-permute-start | bytes 49160 | tf_op jit(solution)/shard_map/ppermute | solution.py:291
  3.9 1.6 %collective-permute-start.1 = (bf16[2,2,16,128]{3,2,1,0:T(8,128)(2,1)S(1)}, bf16[2,2,16,128]{3,2,1,0:T(8,128)(2,1)S(1)}, u32[]{:S(2)}, u32[]{:S(2)}) collective-permute-start(bf16[2,2,16,128]{3,2,1,0:T(8,128)(2,1)S(1)} %get-tuple-element.14), channel_id=1, source_target_pairs={{0,4},{2,6},{4,0},{6,2},{8,12},{10,14},{12,8},{14,10},{1,5},{3,7},... | collective-permute-start | bytes 49160 | tf_op jit(solution)/shard_map/ppermute | solution.py:291
  5.5 0.0 collective-permute-start.2
  6.1 0.0 collective-permute-done.refs_1_
  6.1 1.5 %collective-permute-done.1.refs_2_ = bf16[2,2,16,128]{3,2,1,0:T(8,128)(2,1)S(1)} collective-permute-done((bf16[2,2,16,128]{3,2,1,0:T(8,128)(2,1)S(1)}, bf16[2,2,16,128]{3,2,1,0:T(8,128)(2,1)S(1)}, u32[]{:S(2)}, u32[]{:S(2)}) %collective-permute-start.1) | collective-permute-done | bytes 16416 | tf_op jit(solution)/shard_map/ppermute | solution.py:291
  7.7 2.4 %collective-permute-done.2.refs_3_ = bf16[2,2,16,128]{3,2,1,0:T(8,128)(2,1)S(1)} collective-permute-done((bf16[2,2,16,128]{3,2,1,0:T(8,128)(2,1)S(1)}, bf16[2,2,16,128]{3,2,1,0:T(8,128)(2,1)S(1)}, u32[]{:S(2)}, u32[]{:S(2)}) %collective-permute-start.2) | collective-permute-done | bytes 16416 | tf_op jit(solution)/shard_map/ppermute | solution.py:291
  10.1 0.0 slice-start.2
  10.1 0.0 slice-start.3
  10.2 2.8 %collective-permute-start.3 = (bf16[352,128]{1,0:T(8,128)(2,1)S(1)}, bf16[352,128]{1,0:T(8,128)(2,1)S(1)}, u32[]{:S(2)}, u32[]{:S(2)}) collective-permute-start(bf16[352,128]{1,0:T(8,128)(2,1)S(1)} %shard_map.83), channel_id=1, source_target_pairs={{0,8},{2,10},{4,12},{6,14},{8,0},{10,2},{12,4},{14,6},{1,9},{3,11}... | collective-permute-start | bytes 270344 | tf_op jit(solution)/shard_map/ppermute | solution.py:357
  13.0 3.5 %collective-permute-done.3.refs_6_ = bf16[352,128]{1,0:T(8,128)(2,1)S(1)} collective-permute-done((bf16[352,128]{1,0:T(8,128)(2,1)S(1)}, bf16[352,128]{1,0:T(8,128)(2,1)S(1)}, u32[]{:S(2)}, u32[]{:S(2)}) %collective-permute-start.3) | collective-permute-done | bytes 90144 | tf_op jit(solution)/shard_map/ppermute | solution.py:357
  16.5 0.8 %shard_map.84.refs_0_ = bf16[2,64,128]{2,1,0:T(8,128)(2,1)S(1)} custom-call(bf16[2,2,16,128]{3,2,1,0:T(8,128)(2,1)S(1)} %get-tuple-element.12.refs_0_, bf16[2,2,16,128]{3,2,1,0:T(8,128)(2,1)S(1)} %collective-permute-done.refs_1_, bf16[2,2,16,128]{3,2,1,0:T(8,128)(2,1)S(1)} %collective-permute-done.1.refs_2_, ...), custom_call_target="tpu_custom_call" | custom-call | flops 10000000000 | bytes 1048576 | tf_op jit(solution)/shard_map/pallas_call | solution.py:358
  17.3 0.0 collective-permute-start.6
  17.3 1.7 %collective-permute-start.5 = (bf16[2,64,128]{2,1,0:T(8,128)(2,1)S(1)}, bf16[2,64,128]{2,1,0:T(8,128)(2,1)S(1)}, u32[]{:S(2)}, u32[]{:S(2)}) collective-permute-start(bf16[2,64,128]{2,1,0:T(8,128)(2,1)S(1)} %shard_map.84.refs_0_), channel_id=1, source_target_pairs={{0,4},{2,6},{4,0},{6,2},{8,12},{10,14},{12,8},{14,10},{1,5},{3,7},... | collective-permute-start | bytes 98312 | tf_op jit(solution)/shard_map/ppermute | solution.py:291
  19.1 1.7 %collective-permute-start.4 = (bf16[2,64,128]{2,1,0:T(8,128)(2,1)S(1)}, bf16[2,64,128]{2,1,0:T(8,128)(2,1)S(1)}, u32[]{:S(2)}, u32[]{:S(2)}) collective-permute-start(bf16[2,64,128]{2,1,0:T(8,128)(2,1)S(1)} %shard_map.84.refs_0_), channel_id=1, source_target_pairs={{0,2},{2,0},{4,6},{6,4},{8,10},{10,8},{12,14},{14,12},{1,3},{3,1},... | collective-permute-start | bytes 98312 | tf_op jit(solution)/shard_map/ppermute | solution.py:291
  20.8 1.3 %collective-permute-done.6.refs_3_ = bf16[2,64,128]{2,1,0:T(8,128)(2,1)S(1)} collective-permute-done((bf16[2,64,128]{2,1,0:T(8,128)(2,1)S(1)}, bf16[2,64,128]{2,1,0:T(8,128)(2,1)S(1)}, u32[]{:S(2)}, u32[]{:S(2)}) %collective-permute-start.6) | collective-permute-done | bytes 32800 | tf_op jit(solution)/shard_map/ppermute | solution.py:291
  22.1 0.0 collective-permute-done.5.refs_2_
  22.1 0.8 %collective-permute-done.4.refs_1_ = bf16[2,64,128]{2,1,0:T(8,128)(2,1)S(1)} collective-permute-done((bf16[2,64,128]{2,1,0:T(8,128)(2,1)S(1)}, bf16[2,64,128]{2,1,0:T(8,128)(2,1)S(1)}, u32[]{:S(2)}, u32[]{:S(2)}) %collective-permute-start.4) | collective-permute-done | bytes 32800 | tf_op jit(solution)/shard_map/ppermute | solution.py:291
  23.0 0.0 slice-done.2
  23.0 0.0 slice-done.3
  23.0 2.3 %shard_map.85 = (f32[2,4,1024]{2,1,0:T(4,128)S(1)}, f32[2,4,1024]{2,1,0:T(4,128)S(1)}) custom-call(bf16[2,64,128]{2,1,0:T(8,128)(2,1)S(1)} %shard_map.84.refs_0_, bf16[2,64,128]{2,1,0:T(8,128)(2,1)S(1)} %collective-permute-done.4.refs_1_, bf16[2,64,128]{2,1,0:T(8,128)(2,1)S(1)} %collective-permute-done.5.refs_2_, ...), custom_call_target="tpu_custom_call" | custom-call | tf_op jit(solution)/shard_map/pallas_call | solution.py:368
  25.3 0.0 collective-permute-start.7
  25.3 1.2 %collective-permute-done.7 = f32[2,4,1024]{2,1,0:T(4,128)S(1)} collective-permute-done((f32[2,4,1024]{2,1,0:T(4,128)S(1)}, f32[2,4,1024]{2,1,0:T(4,128)S(1)}, u32[]{:S(2)}, u32[]{:S(2)}) %collective-permute-start.7) | collective-permute-done | bytes 32800 | tf_op jit(solution)/shard_map/ppermute | solution.py:376
  26.5 0.6 %add_convert_fusion = bf16[2,4,1024]{2,1,0:T(4,128)(2,1)} fusion(f32[2,4,1024]{2,1,0:T(4,128)S(1)} %get-tuple-element.17, f32[2,4,1024]{2,1,0:T(4,128)S(1)} %collective-permute-done.7), kind=kLoop, calls=%fused_computation | loop fusion | flops 16384 | bytes 81920 | tf_op jit(solution)/shard_map/convert_element_type | solution.py:377
  (7 shorter events, 0.0 us)
Async XLA Ops:
  0.9 5.3 %collective-permute-start = (bf16[2,2,16,128]{3,2,1,0:T(8,128)(2,1)S(1)}, bf16[2,2,16,128]{3,2,1,0:T(8,128)(2,1)S(1)}, u32[]{:S(2)}, u32[]{:S(2)}) collective-permute-start(bf16[2,2,16,128]{3,2,1,0:T(8,128)(2,1)S(1)} %get-tuple-element.13), channel_id=1, source_target_pairs={{0,2},{2,0},{4,6},{6,4},{8,10},{10,8},{12,14},{14,12},{1,3},{3,1},... | collective-permute-start | bytes 49160 | tf_op jit(solution)/shard_map/ppermute | solution.py:291
  3.9 3.8 %collective-permute-start.1 = (bf16[2,2,16,128]{3,2,1,0:T(8,128)(2,1)S(1)}, bf16[2,2,16,128]{3,2,1,0:T(8,128)(2,1)S(1)}, u32[]{:S(2)}, u32[]{:S(2)}) collective-permute-start(bf16[2,2,16,128]{3,2,1,0:T(8,128)(2,1)S(1)} %get-tuple-element.14), channel_id=1, source_target_pairs={{0,4},{2,6},{4,0},{6,2},{8,12},{10,14},{12,8},{14,10},{1,5},{3,7},... | collective-permute-start | bytes 49160 | tf_op jit(solution)/shard_map/ppermute | solution.py:291
  5.5 4.6 %collective-permute-start.2 = (bf16[2,2,16,128]{3,2,1,0:T(8,128)(2,1)S(1)}, bf16[2,2,16,128]{3,2,1,0:T(8,128)(2,1)S(1)}, u32[]{:S(2)}, u32[]{:S(2)}) collective-permute-start(bf16[2,2,16,128]{3,2,1,0:T(8,128)(2,1)S(1)} %get-tuple-element.15), channel_id=1, source_target_pairs={{0,6},{2,4},{4,2},{6,0},{8,14},{10,12},{12,10},{14,8},{1,7},{3,5},... | collective-permute-start | bytes 49160 | tf_op jit(solution)/shard_map/ppermute | solution.py:291
  10.1 12.9 %slice-start = ((s8[16777216]{0:T(1024)(128)(4,1)}), s8[4194304]{0:T(1024)(128)(4,1)S(1)}, s32[]{:S(2)}) async-start(s8[16777216]{0:T(1024)(128)(4,1)} %bitcast.6), calls=%async_computation | async-start | bytes 8388608
  10.1 12.9 %slice-start.1 = ((s8[16777216]{0:T(1024)(128)(4,1)}), s8[4194304]{0:T(1024)(128)(4,1)S(1)}, s32[]{:S(2)}) async-start(s8[16777216]{0:T(1024)(128)(4,1)} %bitcast.6), calls=%async_computation.1 | async-start | bytes 8388608
  10.1 12.9 %slice-start.2 = ((s8[16777216]{0:T(1024)(128)(4,1)}), s8[4194304]{0:T(1024)(128)(4,1)S(1)}, s32[]{:S(2)}) async-start(s8[16777216]{0:T(1024)(128)(4,1)} %bitcast.6), calls=%async_computation.2 | async-start | bytes 8388608
  10.1 12.8 %slice-start.3 = ((s8[16777216]{0:T(1024)(128)(4,1)}), s8[4194304]{0:T(1024)(128)(4,1)S(1)}, s32[]{:S(2)}) async-start(s8[16777216]{0:T(1024)(128)(4,1)} %bitcast.6), calls=%async_computation.3 | async-start | bytes 8388608
  10.2 6.3 %collective-permute-start.3 = (bf16[352,128]{1,0:T(8,128)(2,1)S(1)}, bf16[352,128]{1,0:T(8,128)(2,1)S(1)}, u32[]{:S(2)}, u32[]{:S(2)}) collective-permute-start(bf16[352,128]{1,0:T(8,128)(2,1)S(1)} %shard_map.83), channel_id=1, source_target_pairs={{0,8},{2,10},{4,12},{6,14},{8,0},{10,2},{12,4},{14,6},{1,9},{3,11}... | collective-permute-start | bytes 270344 | tf_op jit(solution)/shard_map/ppermute | solution.py:357
  17.3 4.9 %collective-permute-start.6 = (bf16[2,64,128]{2,1,0:T(8,128)(2,1)S(1)}, bf16[2,64,128]{2,1,0:T(8,128)(2,1)S(1)}, u32[]{:S(2)}, u32[]{:S(2)}) collective-permute-start(bf16[2,64,128]{2,1,0:T(8,128)(2,1)S(1)} %shard_map.84.refs_0_), channel_id=1, source_target_pairs={{0,6},{2,4},{4,2},{6,0},{8,14},{10,12},{12,10},{14,8},{1,7},{3,5},... | collective-permute-start | bytes 98312 | tf_op jit(solution)/shard_map/ppermute | solution.py:291
  17.3 4.8 %collective-permute-start.5 = (bf16[2,64,128]{2,1,0:T(8,128)(2,1)S(1)}, bf16[2,64,128]{2,1,0:T(8,128)(2,1)S(1)}, u32[]{:S(2)}, u32[]{:S(2)}) collective-permute-start(bf16[2,64,128]{2,1,0:T(8,128)(2,1)S(1)} %shard_map.84.refs_0_), channel_id=1, source_target_pairs={{0,4},{2,6},{4,0},{6,2},{8,12},{10,14},{12,8},{14,10},{1,5},{3,7},... | collective-permute-start | bytes 98312 | tf_op jit(solution)/shard_map/ppermute | solution.py:291
  19.1 3.9 %collective-permute-start.4 = (bf16[2,64,128]{2,1,0:T(8,128)(2,1)S(1)}, bf16[2,64,128]{2,1,0:T(8,128)(2,1)S(1)}, u32[]{:S(2)}, u32[]{:S(2)}) collective-permute-start(bf16[2,64,128]{2,1,0:T(8,128)(2,1)S(1)} %shard_map.84.refs_0_), channel_id=1, source_target_pairs={{0,2},{2,0},{4,6},{6,4},{8,10},{10,8},{12,14},{14,12},{1,3},{3,1},... | collective-permute-start | bytes 98312 | tf_op jit(solution)/shard_map/ppermute | solution.py:291
  25.3 1.2 %collective-permute-start.7 = (f32[2,4,1024]{2,1,0:T(4,128)S(1)}, f32[2,4,1024]{2,1,0:T(4,128)S(1)}, u32[]{:S(2)}, u32[]{:S(2)}) collective-permute-start(f32[2,4,1024]{2,1,0:T(4,128)S(1)} %get-tuple-element.18), channel_id=1, source_target_pairs={{0,1},{1,0},{2,3},{3,2},{4,5},{5,4},{6,7},{7,6},{8,9},{9,8},{10,11... | collective-permute-start | bytes 98312 | tf_op jit(solution)/shard_map/ppermute | solution.py:376

commit v5 on v4

--- a/solution.py
+++ b/solution.py
@@ -117,31 +117,17 @@
         other_ref[layer] = jnp.where(first, high, low)
 
 
-def softmax_context(queries, new_keys, new_values, keys, values, allowed, groups):
-    rows, depth = queries.shape
-    grouped = (groups, rows // groups, depth)
-    scaling = depth ** (-0.5)
+def softmax_context(queries, keys, values, allowed):
+    _, depth = queries.shape
     scores = lax.dot_general(
         queries, keys, (((1,), (1,)), ((), ())), preferred_element_type=jnp.float32
     )
-    scores = jnp.where(allowed, scores.reshape(allowed.shape) * scaling, -1e30)
-    new_keys = new_keys.astype(jnp.float32)[:, None, :]
-    own_score = jnp.sum(
-        queries.astype(jnp.float32).reshape(grouped) * new_keys, axis=-1, keepdims=True
-    )
-    own_score = own_score * scaling
-    peak = jnp.maximum(jnp.max(scores, axis=-1, keepdims=True), own_score)
+    scores = jnp.where(allowed, scores * depth ** (-0.5), -1e30)
+    peak = jnp.max(scores, axis=-1, keepdims=True)
     raised = jnp.exp(scores - peak)
-    own_raised = jnp.exp(own_score - peak)
-    denominator = jnp.sum(raised, axis=-1, keepdims=True) + own_raised
-    weights = (raised / denominator).astype(jnp.bfloat16)
-    own_weight = (own_raised / denominator).astype(jnp.bfloat16)
-    context = jnp.dot(
-        weights.reshape(rows, keys.shape[0]), values, preferred_element_type=jnp.float32
-    ).reshape(grouped)
-    new_values = new_values.astype(jnp.float32)[:, None, :]
-    context = context + own_weight.astype(jnp.float32) * new_values
-    return context.astype(jnp.bfloat16).reshape(rows, depth)
+    denominator = jnp.sum(raised, axis=-1, keepdims=True)
+    context = jnp.dot(raised.astype(jnp.bfloat16), values, preferred_element_type=jnp.float32)
+    return (context / denominator).astype(jnp.bfloat16)
 
 
 def place(pairs):
@@ -205,15 +191,17 @@
     positions = block // groups
     per_block = 4 * block
     sources = 2 * pairs
-    shape = (groups, query_rows // groups, sources * block)
-    group = lax.broadcasted_iota(jnp.int32, shape, 0)
-    column = lax.broadcasted_iota(jnp.int32, shape, 2)
+    cached = sources * block
+    shape = (query_rows, cached + groups)
+    group = lax.broadcasted_iota(jnp.int32, shape, 0) // (query_rows // groups)
+    column = lax.broadcasted_iota(jnp.int32, shape, 1)
     within = column % block
     column_group = (within // (positions * kv_heads)) * kv_heads + within % kv_heads
     source = column // block
     source = ((source // pairs) ^ mine) * pairs + ((source % pairs) ^ pair)
     position = source * positions + (within // kv_heads) % positions
-    same_group = column_group == group
+    position = jnp.where(column < cached, position, -1).astype(jnp.float32)
+    same_group = jnp.where(column < cached, column_group, column - cached) == group
     tail = pairs * per_block
 
     def side_rows(sequence, first, count):
@@ -231,20 +219,17 @@
                     + [
                         partner_ref[k * per_block + first : k * per_block + first + block, :]
                         for k in range(pairs)
-                    ],
+                    ]
+                    + [side_rows(sequence, query_rows + which * groups, groups)],
                     axis=0,
                 )
             )
-        queries = side_rows(sequence, 0, query_rows)
-        new_keys = side_rows(sequence, query_rows, groups)
-        new_values = side_rows(sequence, query_rows + groups, groups)
         limit = jnp.where(
             mine == sequence, limit_ref[...], partner_ref[tail + query_rows + 2 * groups :, :]
         )
-        limit = limit[:1, :1].astype(jnp.float32)
-        allowed = same_group & (position.astype(jnp.float32) < limit[None])
+        allowed = same_group & (position < limit[:1, :1].astype(jnp.float32))
         out_ref[sequence] = softmax_context(
-            queries, new_keys, new_values, stacked[0], stacked[1], allowed, groups
+            side_rows(sequence, 0, query_rows), stacked[0], stacked[1], allowed
         )
 
 

time: 27.3 us -> 27.2 us (level)
  no operation moved by 1% of the time
where the time goes in v5:
time: 27.2 us; the launch traced here: 27 us
  starting transfers between devices  11 us (40%)
  waiting for transfers between devices  10.9 us (40%)
  Pallas kernels  3.75 us (14%)
  between operations  0.74 us (3%)
  other arithmetic  0.62 us (2%)
    ppermute x6, starting transfers between devices, exchange(): lax.ppermute(blocks[k], 'seq', [(i, i ^ k) for i in range(count)])  8.16 us
    ppermute x6, waiting for transfers between devices, exchange(): lax.ppermute(blocks[k], 'seq', [(i, i ^ k) for i in range(count)])  6.15 us
    ppermute x1, waiting for transfers between devices, by_pairs(): lax.ppermute(packed, 'seq', [(i, i ^ pairs) for i in range(sequences)])  3.52 us
    ppermute x1, starting transfers between devices, by_pairs(): lax.ppermute(packed, 'seq', [(i, i ^ pairs) for i in range(sequences)])  2.82 us
    pallas_call x1, Pallas kernels, by_pairs(): pl.pallas_call(functools.partial(pair_project_kernel, pairs, layers, 4 *...  2.27 us
    ppermute x1, waiting for transfers between devices, by_pairs(): arrived = lax.ppermute(other, 'head', [(0, 1), (1, 0)])  1.22 us
    pallas_call x1, Pallas kernels, by_pairs(): pl.pallas_call(functools.partial(stage_kernel, pairs), out_shape=[block_s...  0.85 us
    pallas_call x1, Pallas kernels, by_pairs(): pl.pallas_call(functools.partial(pair_attend_kernel, pairs, layers, kv_he...  0.62 us
  transfers between devices with their start and end apart: 8, of which 6 were waited for; matrix products, arithmetic and copies ran while one was open for 0% of the time, Pallas kernels for 0%

profile of v5, /device:TPU:0, one launch (start us, length us, event | category | flops | bytes accessed | tf_op | source)
XLA Modules:
  0.0 27.0 jit_solution(711146277674028630)
XLA Ops:
  0.0 0.8 %shard_map.82 = (bf16[2,2,16,128]{3,2,1,0:T(8,128)(2,1)S(1)}, bf16[2,2,16,128]{3,2,1,0:T(8,128)(2,1)S(1)}, bf16[2,2,16,128]{3,2,1,0:T(8,128)(2,1)S(1)}, bf16[2,2...) custom-call(s32[8]{0:T(128)} %slot_hbm.1, bf16[2,8,8,128]{3,2,1,0:T(8,128)(2,1)} %bitcast.8, ...), custom_call_target="tpu_custom_call" | custom-call | flops 10000000000 | bytes 1048576 | tf_op jit(solution)/shard_map/pallas_call | solution.py:309
  0.9 3.0 %collective-permute-start = (bf16[2,2,16,128]{3,2,1,0:T(8,128)(2,1)S(1)}, bf16[2,2,16,128]{3,2,1,0:T(8,128)(2,1)S(1)}, u32[]{:S(2)}, u32[]{:S(2)}) collective-permute-start(bf16[2,2,16,128]{3,2,1,0:T(8,128)(2,1)S(1)} %get-tuple-element.13), channel_id=1, source_target_pairs={{0,2},{2,0},{4,6},{6,4},{8,10},{10,8},{12,14},{14,12},{1,3},{3,1},... | collective-permute-start | bytes 49160 | tf_op jit(solution)/shard_map/ppermute | solution.py:276
  3.9 1.6 %collective-permute-start.1 = (bf16[2,2,16,128]{3,2,1,0:T(8,128)(2,1)S(1)}, bf16[2,2,16,128]{3,2,1,0:T(8,128)(2,1)S(1)}, u32[]{:S(2)}, u32[]{:S(2)}) collective-permute-start(bf16[2,2,16,128]{3,2,1,0:T(8,128)(2,1)S(1)} %get-tuple-element.14), channel_id=1, source_target_pairs={{0,4},{2,6},{4,0},{6,2},{8,12},{10,14},{12,8},{14,10},{1,5},{3,7},... | collective-permute-start | bytes 49160 | tf_op jit(solution)/shard_map/ppermute | solution.py:276
  5.5 0.0 collective-permute-start.2
  6.1 0.0 collective-permute-done.refs_1_
  6.1 1.5 %collective-permute-done.1.refs_2_ = bf16[2,2,16,128]{3,2,1,0:T(8,128)(2,1)S(1)} collective-permute-done((bf16[2,2,16,128]{3,2,1,0:T(8,128)(2,1)S(1)}, bf16[2,2,16,128]{3,2,1,0:T(8,128)(2,1)S(1)}, u32[]{:S(2)}, u32[]{:S(2)}) %collective-permute-start.1) | collective-permute-done | bytes 16416 | tf_op jit(solution)/shard_map/ppermute | solution.py:276
  7.7 2.4 %collective-permute-done.2.refs_3_ = bf16[2,2,16,128]{3,2,1,0:T(8,128)(2,1)S(1)} collective-permute-done((bf16[2,2,16,128]{3,2,1,0:T(8,128)(2,1)S(1)}, bf16[2,2,16,128]{3,2,1,0:T(8,128)(2,1)S(1)}, u32[]{:S(2)}, u32[]{:S(2)}) %collective-permute-start.2) | collective-permute-done | bytes 16416 | tf_op jit(solution)/shard_map/ppermute | solution.py:276
  10.1 0.0 slice-start.2
  10.1 0.0 slice-start.3
  10.2 2.8 %collective-permute-start.3 = (bf16[352,128]{1,0:T(8,128)(2,1)S(1)}, bf16[352,128]{1,0:T(8,128)(2,1)S(1)}, u32[]{:S(2)}, u32[]{:S(2)}) collective-permute-start(bf16[352,128]{1,0:T(8,128)(2,1)S(1)} %shard_map.83), channel_id=1, source_target_pairs={{0,8},{2,10},{4,12},{6,14},{8,0},{10,2},{12,4},{14,6},{1,9},{3,11}... | collective-permute-start | bytes 270344 | tf_op jit(solution)/shard_map/ppermute | solution.py:342
  13.0 3.5 %collective-permute-done.3.refs_6_ = bf16[352,128]{1,0:T(8,128)(2,1)S(1)} collective-permute-done((bf16[352,128]{1,0:T(8,128)(2,1)S(1)}, bf16[352,128]{1,0:T(8,128)(2,1)S(1)}, u32[]{:S(2)}, u32[]{:S(2)}) %collective-permute-start.3) | collective-permute-done | bytes 90144 | tf_op jit(solution)/shard_map/ppermute | solution.py:342
  16.5 0.6 %shard_map.84.refs_0_ = bf16[2,64,128]{2,1,0:T(8,128)(2,1)S(1)} custom-call(bf16[2,2,16,128]{3,2,1,0:T(8,128)(2,1)S(1)} %get-tuple-element.12.refs_0_, bf16[2,2,16,128]{3,2,1,0:T(8,128)(2,1)S(1)} %collective-permute-done.refs_1_, bf16[2,2,16,128]{3,2,1,0:T(8,128)(2,1)S(1)} %collective-permute-done.1.refs_2_, ...), custom_call_target="tpu_custom_call" | custom-call | flops 10000000000 | bytes 1048576 | tf_op jit(solution)/shard_map/pallas_call | solution.py:343
  17.1 0.1 collective-permute-start.6
  17.2 1.7 %collective-permute-start.5 = (bf16[2,64,128]{2,1,0:T(8,128)(2,1)S(1)}, bf16[2,64,128]{2,1,0:T(8,128)(2,1)S(1)}, u32[]{:S(2)}, u32[]{:S(2)}) collective-permute-start(bf16[2,64,128]{2,1,0:T(8,128)(2,1)S(1)} %shard_map.84.refs_0_), channel_id=1, source_target_pairs={{0,4},{2,6},{4,0},{6,2},{8,12},{10,14},{12,8},{14,10},{1,5},{3,7},... | collective-permute-start | bytes 98312 | tf_op jit(solution)/shard_map/ppermute | solution.py:276
  18.9 1.7 %collective-permute-start.4 = (bf16[2,64,128]{2,1,0:T(8,128)(2,1)S(1)}, bf16[2,64,128]{2,1,0:T(8,128)(2,1)S(1)}, u32[]{:S(2)}, u32[]{:S(2)}) collective-permute-start(bf16[2,64,128]{2,1,0:T(8,128)(2,1)S(1)} %shard_map.84.refs_0_), channel_id=1, source_target_pairs={{0,2},{2,0},{4,6},{6,4},{8,10},{10,8},{12,14},{14,12},{1,3},{3,1},... | collective-permute-start | bytes 98312 | tf_op jit(solution)/shard_map/ppermute | solution.py:276
  20.7 1.3 %collective-permute-done.6.refs_3_ = bf16[2,64,128]{2,1,0:T(8,128)(2,1)S(1)} collective-permute-done((bf16[2,64,128]{2,1,0:T(8,128)(2,1)S(1)}, bf16[2,64,128]{2,1,0:T(8,128)(2,1)S(1)}, u32[]{:S(2)}, u32[]{:S(2)}) %collective-permute-start.6) | collective-permute-done | bytes 32800 | tf_op jit(solution)/shard_map/ppermute | solution.py:276
  22.0 0.0 collective-permute-done.5.refs_2_
  22.0 0.8 %collective-permute-done.4.refs_1_ = bf16[2,64,128]{2,1,0:T(8,128)(2,1)S(1)} collective-permute-done((bf16[2,64,128]{2,1,0:T(8,128)(2,1)S(1)}, bf16[2,64,128]{2,1,0:T(8,128)(2,1)S(1)}, u32[]{:S(2)}, u32[]{:S(2)}) %collective-permute-start.4) | collective-permute-done | bytes 32800 | tf_op jit(solution)/shard_map/ppermute | solution.py:276
  22.9 0.0 slice-done
  22.9 0.0 slice-done.1
  22.9 2.3 %shard_map.85 = (f32[2,4,1024]{2,1,0:T(4,128)S(1)}, f32[2,4,1024]{2,1,0:T(4,128)S(1)}) custom-call(bf16[2,64,128]{2,1,0:T(8,128)(2,1)S(1)} %shard_map.84.refs_0_, bf16[2,64,128]{2,1,0:T(8,128)(2,1)S(1)} %collective-permute-done.4.refs_1_, bf16[2,64,128]{2,1,0:T(8,128)(2,1)S(1)} %collective-permute-done.5.refs_2_, ...), custom_call_target="tpu_custom_call" | custom-call | tf_op jit(solution)/shard_map/pallas_call | solution.py:353
  25.2 0.0 collective-permute-start.7
  25.2 1.2 %collective-permute-done.7 = f32[2,4,1024]{2,1,0:T(4,128)S(1)} collective-permute-done((f32[2,4,1024]{2,1,0:T(4,128)S(1)}, f32[2,4,1024]{2,1,0:T(4,128)S(1)}, u32[]{:S(2)}, u32[]{:S(2)}) %collective-permute-start.7) | collective-permute-done | bytes 32800 | tf_op jit(solution)/shard_map/ppermute | solution.py:361
  26.4 0.6 %add_convert_fusion = bf16[2,4,1024]{2,1,0:T(4,128)(2,1)} fusion(f32[2,4,1024]{2,1,0:T(4,128)S(1)} %get-tuple-element.17, f32[2,4,1024]{2,1,0:T(4,128)S(1)} %collective-permute-done.7), kind=kLoop, calls=%fused_computation | loop fusion | flops 16384 | bytes 81920 | tf_op jit(solution)/shard_map/convert_element_type | solution.py:362
  (7 shorter events, 0.0 us)
Async XLA Ops:
  0.9 5.3 %collective-permute-start = (bf16[2,2,16,128]{3,2,1,0:T(8,128)(2,1)S(1)}, bf16[2,2,16,128]{3,2,1,0:T(8,128)(2,1)S(1)}, u32[]{:S(2)}, u32[]{:S(2)}) collective-permute-start(bf16[2,2,16,128]{3,2,1,0:T(8,128)(2,1)S(1)} %get-tuple-element.13), channel_id=1, source_target_pairs={{0,2},{2,0},{4,6},{6,4},{8,10},{10,8},{12,14},{14,12},{1,3},{3,1},... | collective-permute-start | bytes 49160 | tf_op jit(solution)/shard_map/ppermute | solution.py:276
  3.9 3.8 %collective-permute-start.1 = (bf16[2,2,16,128]{3,2,1,0:T(8,128)(2,1)S(1)}, bf16[2,2,16,128]{3,2,1,0:T(8,128)(2,1)S(1)}, u32[]{:S(2)}, u32[]{:S(2)}) collective-permute-start(bf16[2,2,16,128]{3,2,1,0:T(8,128)(2,1)S(1)} %get-tuple-element.14), channel_id=1, source_target_pairs={{0,4},{2,6},{4,0},{6,2},{8,12},{10,14},{12,8},{14,10},{1,5},{3,7},... | collective-permute-start | bytes 49160 | tf_op jit(solution)/shard_map/ppermute | solution.py:276
  5.5 4.6 %collective-permute-start.2 = (bf16[2,2,16,128]{3,2,1,0:T(8,128)(2,1)S(1)}, bf16[2,2,16,128]{3,2,1,0:T(8,128)(2,1)S(1)}, u32[]{:S(2)}, u32[]{:S(2)}) collective-permute-start(bf16[2,2,16,128]{3,2,1,0:T(8,128)(2,1)S(1)} %get-tuple-element.15), channel_id=1, source_target_pairs={{0,6},{2,4},{4,2},{6,0},{8,14},{10,12},{12,10},{14,8},{1,7},{3,5},... | collective-permute-start | bytes 49160 | tf_op jit(solution)/shard_map/ppermute | solution.py:276
  10.1 12.8 %slice-start = ((s8[16777216]{0:T(1024)(128)(4,1)}), s8[4194304]{0:T(1024)(128)(4,1)S(1)}, s32[]{:S(2)}) async-start(s8[16777216]{0:T(1024)(128)(4,1)} %bitcast.6), calls=%async_computation | async-start | bytes 8388608
  10.1 12.8 %slice-start.1 = ((s8[16777216]{0:T(1024)(128)(4,1)}), s8[4194304]{0:T(1024)(128)(4,1)S(1)}, s32[]{:S(2)}) async-start(s8[16777216]{0:T(1024)(128)(4,1)} %bitcast.6), calls=%async_computation.1 | async-start | bytes 8388608
  10.1 12.7 %slice-start.2 = ((s8[16777216]{0:T(1024)(128)(4,1)}), s8[4194304]{0:T(1024)(128)(4,1)S(1)}, s32[]{:S(2)}) async-start(s8[16777216]{0:T(1024)(128)(4,1)} %bitcast.6), calls=%async_computation.2 | async-start | bytes 8388608
  10.1 12.7 %slice-start.3 = ((s8[16777216]{0:T(1024)(128)(4,1)}), s8[4194304]{0:T(1024)(128)(4,1)S(1)}, s32[]{:S(2)}) async-start(s8[16777216]{0:T(1024)(128)(4,1)} %bitcast.6), calls=%async_computation.3 | async-start | bytes 8388608
  10.2 6.3 %collective-permute-start.3 = (bf16[352,128]{1,0:T(8,128)(2,1)S(1)}, bf16[352,128]{1,0:T(8,128)(2,1)S(1)}, u32[]{:S(2)}, u32[]{:S(2)}) collective-permute-start(bf16[352,128]{1,0:T(8,128)(2,1)S(1)} %shard_map.83), channel_id=1, source_target_pairs={{0,8},{2,10},{4,12},{6,14},{8,0},{10,2},{12,4},{14,6},{1,9},{3,11}... | collective-permute-start | bytes 270344 | tf_op jit(solution)/shard_map/ppermute | solution.py:342
  17.1 4.9 %collective-permute-start.6 = (bf16[2,64,128]{2,1,0:T(8,128)(2,1)S(1)}, bf16[2,64,128]{2,1,0:T(8,128)(2,1)S(1)}, u32[]{:S(2)}, u32[]{:S(2)}) collective-permute-start(bf16[2,64,128]{2,1,0:T(8,128)(2,1)S(1)} %shard_map.84.refs_0_), channel_id=1, source_target_pairs={{0,6},{2,4},{4,2},{6,0},{8,14},{10,12},{12,10},{14,8},{1,7},{3,5},... | collective-permute-start | bytes 98312 | tf_op jit(solution)/shard_map/ppermute | solution.py:276
  17.2 4.8 %collective-permute-start.5 = (bf16[2,64,128]{2,1,0:T(8,128)(2,1)S(1)}, bf16[2,64,128]{2,1,0:T(8,128)(2,1)S(1)}, u32[]{:S(2)}, u32[]{:S(2)}) collective-permute-start(bf16[2,64,128]{2,1,0:T(8,128)(2,1)S(1)} %shard_map.84.refs_0_), channel_id=1, source_target_pairs={{0,4},{2,6},{4,0},{6,2},{8,12},{10,14},{12,8},{14,10},{1,5},{3,7},... | collective-permute-start | bytes 98312 | tf_op jit(solution)/shard_map/ppermute | solution.py:276
  18.9 3.9 %collective-permute-start.4 = (bf16[2,64,128]{2,1,0:T(8,128)(2,1)S(1)}, bf16[2,64,128]{2,1,0:T(8,128)(2,1)S(1)}, u32[]{:S(2)}, u32[]{:S(2)}) collective-permute-start(bf16[2,64,128]{2,1,0:T(8,128)(2,1)S(1)} %shard_map.84.refs_0_), channel_id=1, source_target_pairs={{0,2},{2,0},{4,6},{6,4},{8,10},{10,8},{12,14},{14,12},{1,3},{3,1},... | collective-permute-start | bytes 98312 | tf_op jit(solution)/shard_map/ppermute | solution.py:276
  25.2 1.2 %collective-permute-start.7 = (f32[2,4,1024]{2,1,0:T(4,128)S(1)}, f32[2,4,1024]{2,1,0:T(4,128)S(1)}, u32[]{:S(2)}, u32[]{:S(2)}) collective-permute-start(f32[2,4,1024]{2,1,0:T(4,128)S(1)} %get-tuple-element.18), channel_id=1, source_target_pairs={{0,1},{1,0},{2,3},{3,2},{4,5},{5,4},{6,7},{7,6},{8,9},{9,8},{10,11... | collective-permute-start | bytes 98312 | tf_op jit(solution)/shard_map/ppermute | solution.py:361

commit v6 on v5

--- a/solution.py
+++ b/solution.py
@@ -135,32 +135,15 @@
     return index % pairs, index // pairs
 
 
-def stage_kernel(
-    pairs,
-    slot_hbm,
-    keys_hbm,
-    values_hbm,
-    queries_hbm,
-    new_keys_hbm,
-    new_values_hbm,
-    *refs,
-):
-    blocks, side_ref = refs[:pairs], refs[pairs]
-    slots, keys, values, sem = refs[pairs + 1 :]
+def stage_kernel(pairs, slot_hbm, keys_hbm, values_hbm, *refs):
+    blocks, (slots, keys, values, sem) = refs[:pairs], refs[pairs:]
     layers, _, rows, _ = keys.shape
-    query_rows, new_rows = queries_hbm.shape[0], new_keys_hbm.shape[0]
-    sources = (slot_hbm, keys_hbm, values_hbm, queries_hbm, new_keys_hbm, new_values_hbm)
-    targets = (
-        slots,
-        keys,
-        values,
-        side_ref.at[pl.ds(0, query_rows)],
-        side_ref.at[pl.ds(query_rows, new_rows)],
-        side_ref.at[pl.ds(query_rows + new_rows, new_rows)],
-    )
+    targets = (slots, keys, values)
     copies = [
         pltpu.make_async_copy(source, target, sem.at[i])
-        for i, (source, target) in enumerate(zip(sources, targets, strict=True))
+        for i, (source, target) in enumerate(
+            zip((slot_hbm, keys_hbm, values_hbm), targets, strict=True)
+        )
     ]
     for copy in copies:
         copy.start()
@@ -173,6 +156,18 @@
             for which, held in enumerate((keys, values)):
                 for layer in range(layers):
                     blocks[k][side, which, layer * rows : (layer + 1) * rows, :] = held[layer, slot]
+
+
+def own_rows_kernel(queries_hbm, new_keys_hbm, new_values_hbm, side_ref, sem):
+    copies = []
+    start = 0
+    for i, source in enumerate((queries_hbm, new_keys_hbm, new_values_hbm)):
+        target = side_ref.at[pl.ds(start, source.shape[0])]
+        copies.append(pltpu.make_async_copy(source, target, sem.at[i]))
+        copies[-1].start()
+        start += source.shape[0]
+    for copy in copies:
+        copy.wait()
 
 
 def pack_kernel(*refs):
@@ -306,34 +301,42 @@
     query_rows, groups = layers * heads, layers * kv_heads
     side_rows = query_rows + 2 * groups
     block_shape = jax.ShapeDtypeStruct((2, 2, block, depth), bf16)
-    *blocks, side = pl.pallas_call(
+    blocks = pl.pallas_call(
         functools.partial(stage_kernel, pairs),
-        out_shape=[block_shape] * pairs + [jax.ShapeDtypeStruct((side_rows, depth), bf16)],
-        in_specs=[HBM] * 6,
-        out_specs=[VMEM] * (pairs + 1),
+        out_shape=[block_shape] * pairs,
+        in_specs=[HBM] * 3,
+        out_specs=[VMEM] * pairs,
         scratch_shapes=[
             pltpu.SMEM((sequences,), jnp.int32),
             pltpu.VMEM(flat, bf16),
             pltpu.VMEM(flat, bf16),
-            pltpu.SemaphoreType.DMA((6,)),
+            pltpu.SemaphoreType.DMA((3,)),
         ],
         compiler_params=params(4),
         cost_estimate=COVER,
     )(
+        *in_hbm(slot_index, cache_keys.reshape(flat), prefill_value_cache.reshape(flat)),
+    )
+    blocks = exchange(blocks)
+    side = pl.pallas_call(
+        own_rows_kernel,
+        out_shape=jax.ShapeDtypeStruct((side_rows, depth), bf16),
+        in_specs=[HBM] * 3,
+        out_specs=VMEM,
+        scratch_shapes=[pltpu.SemaphoreType.DMA((3,))],
+        compiler_params=params(4),
+        cost_estimate=COVER,
+    )(
         *in_hbm(
-            slot_index,
-            cache_keys.reshape(flat),
-            prefill_value_cache.reshape(flat),
             queries.reshape(query_rows, depth),
             new_keys.reshape(groups, depth),
             token_value_rows.reshape(groups, depth),
         ),
     )
-    blocks = exchange(blocks)
-    limit = jnp.broadcast_to(lengths.astype(bf16)[:, None], (16, depth))
+    limit = jnp.broadcast_to(lengths.astype(bf16)[:, None], (8, depth))
     packed = pl.pallas_call(
         pack_kernel,
-        out_shape=jax.ShapeDtypeStruct((pairs * 4 * block + side_rows + 16, depth), bf16),
+        out_shape=jax.ShapeDtypeStruct((pairs * 4 * block + side_rows + 8, depth), bf16),
         in_specs=[VMEM] * (pairs + 2),
         out_specs=VMEM,
         compiler_params=params(4),

time: 27.2 us -> 27.2 us (level)
  waiting for transfers between devices: 10.9 us -> 10.1 us
  Pallas kernels: 3.75 us -> 4.47 us
    ppermute x6, waiting for transfers between devices: 6.15 us -> 5.4 us  [exchange(): lax.ppermute(blocks[k], 'seq', [(i, i ^ k) for i in range(count)])]
    pallas_call x0 -> x1, Pallas kernels: none -> 0.75 us  [by_pairs(): pl.pallas_call(own_rows_kernel, out_shape=jax.ShapeDtypeStruct((side_rows...]
  transfers between devices with their start and end apart: 8 -> 8, of which waited for: 6 -> 6; matrix products, arithmetic and copies ran while one was open for 0% -> 0% of each run, Pallas kernels for 0% -> 3%
where the time goes in v6:
time: 27.2 us; the launch traced here: 26.9 us
  starting transfers between devices  11 us (40%)
  waiting for transfers between devices  10.1 us (37%)
  Pallas kernels  4.47 us (16%)
  between operations  0.74 us (3%)
  other arithmetic  0.62 us (2%)
    ppermute x6, starting transfers between devices, exchange(): lax.ppermute(blocks[k], 'seq', [(i, i ^ k) for i in range(count)])  8.16 us
    ppermute x6, waiting for transfers between devices, exchange(): lax.ppermute(blocks[k], 'seq', [(i, i ^ k) for i in range(count)])  5.4 us
    ppermute x1, waiting for transfers between devices, by_pairs(): lax.ppermute(packed, 'seq', [(i, i ^ pairs) for i in range(sequences)])  3.47 us
    ppermute x1, starting transfers between devices, by_pairs(): lax.ppermute(packed, 'seq', [(i, i ^ pairs) for i in range(sequences)])  2.83 us
    pallas_call x1, Pallas kernels, by_pairs(): pl.pallas_call(functools.partial(pair_project_kernel, pairs, layers, 4 *...  2.27 us
    ppermute x1, waiting for transfers between devices, by_pairs(): arrived = lax.ppermute(other, 'head', [(0, 1), (1, 0)])  1.22 us
    pallas_call x1, Pallas kernels, by_pairs(): pl.pallas_call(functools.partial(stage_kernel, pairs), out_shape=[block_s...  0.82 us
    pallas_call x1, Pallas kernels, by_pairs(): pl.pallas_call(own_rows_kernel, out_shape=jax.ShapeDtypeStruct((side_rows...  0.75 us
  transfers between devices with their start and end apart: 8, of which 6 were waited for; matrix products, arithmetic and copies ran while one was open for 0% of the time, Pallas kernels for 3%

profile of v6, /device:TPU:0, one launch (start us, length us, event | category | flops | bytes accessed | tf_op | source)
XLA Modules:
  0.0 26.9 jit_solution(16308395944969909932)
XLA Ops:
  0.0 0.8 %shard_map.82 = (bf16[2,2,16,128]{3,2,1,0:T(8,128)(2,1)S(1)}, bf16[2,2,16,128]{3,2,1,0:T(8,128)(2,1)S(1)}, bf16[2,2,16,128]{3,2,1,0:T(8,128)(2,1)S(1)}, bf16[2,2,16,128]{3,2,1,0:T(8,128)(2,1)S(1)}) custom-call(s32[8]{0:T(128)} %slot_hbm.1, bf16[2,8,8,128]{3,2,1,0:T(8,128)(2,1)} %bitcast.8, bf16[2,8,8,128]{3,2,1,0:T(8,128)(2,1)} %bitcast.9), custom_call_target="tpu_custom_call" | custom-call | flops 10000000000 | bytes 1048576 | tf_op jit(solution)/shard_map/pallas_call | solution.py:304
  0.8 3.0 %collective-permute-start = (bf16[2,2,16,128]{3,2,1,0:T(8,128)(2,1)S(1)}, bf16[2,2,16,128]{3,2,1,0:T(8,128)(2,1)S(1)}, u32[]{:S(2)}, u32[]{:S(2)}) collective-permute-start(bf16[2,2,16,128]{3,2,1,0:T(8,128)(2,1)S(1)} %get-tuple-element.12), channel_id=1, source_target_pairs={{0,2},{2,0},{4,6},{6,4},{8,10},{10,8},{12,14},{14,12},{1,3},{3,1},... | collective-permute-start | bytes 49160 | tf_op jit(solution)/shard_map/ppermute | solution.py:271
  3.9 1.6 %collective-permute-start.1 = (bf16[2,2,16,128]{3,2,1,0:T(8,128)(2,1)S(1)}, bf16[2,2,16,128]{3,2,1,0:T(8,128)(2,1)S(1)}, u32[]{:S(2)}, u32[]{:S(2)}) collective-permute-start(bf16[2,2,16,128]{3,2,1,0:T(8,128)(2,1)S(1)} %get-tuple-element.13), channel_id=1, source_target_pairs={{0,4},{2,6},{4,0},{6,2},{8,12},{10,14},{12,8},{14,10},{1,5},{3,7},... | collective-permute-start | bytes 49160 | tf_op jit(solution)/shard_map/ppermute | solution.py:271
  5.4 0.0 collective-permute-start.2
  5.4 0.7 %shard_map.83.refs_4_ = bf16[80,128]{1,0:T(8,128)(2,1)S(1)} custom-call(bf16[64,128]{1,0:T(8,128)(2,1)} %bitcast.10, bf16[8,128]{1,0:T(8,128)(2,1)} %bitcast.11, bf16[8,128]{1,0:T(8,128)(2,1)} %bitcast.12), custom_call_target="tpu_custom_call" | custom-call | flops 10000000000 | bytes 1048576 | tf_op jit(solution)/shard_map/pallas_call | solution.py:321
  6.8 0.0 collective-permute-done.refs_1_
  6.9 0.8 %collective-permute-done.1.refs_2_ = bf16[2,2,16,128]{3,2,1,0:T(8,128)(2,1)S(1)} collective-permute-done((bf16[2,2,16,128]{3,2,1,0:T(8,128)(2,1)S(1)}, bf16[2,2,16,128]{3,2,1,0:T(8,128)(2,1)S(1)}, u32[]{:S(2)}, u32[]{:S(2)}) %collective-permute-start.1) | collective-permute-done | bytes 16416 | tf_op jit(solution)/shard_map/ppermute | solution.py:271
  7.6 2.4 %collective-permute-done.2.refs_3_ = bf16[2,2,16,128]{3,2,1,0:T(8,128)(2,1)S(1)} collective-permute-done((bf16[2,2,16,128]{3,2,1,0:T(8,128)(2,1)S(1)}, bf16[2,2,16,128]{3,2,1,0:T(8,128)(2,1)S(1)}, u32[]{:S(2)}, u32[]{:S(2)}) %collective-permute-start.2) | collective-permute-done | bytes 16416 | tf_op jit(solution)/shard_map/ppermute | solution.py:271
  10.1 0.0 slice-start.2
  10.1 0.0 slice-start.3
  10.1 2.8 %collective-permute-start.3 = (bf16[344,128]{1,0:T(8,128)(2,1)S(1)}, bf16[344,128]{1,0:T(8,128)(2,1)S(1)}, u32[]{:S(2)}, u32[]{:S(2)}) collective-permute-start(bf16[344,128]{1,0:T(8,128)(2,1)S(1)} %shard_map.84), channel_id=1, source_target_pairs={{0,8},{2,10},{4,12},{6,14},{8,0},{10,2},{12,4},{14,6},{1,9},{3,11}... | collective-permute-start | bytes 264200 | tf_op jit(solution)/shard_map/ppermute | solution.py:345
  12.9 3.5 %collective-permute-done.3.refs_6_ = bf16[344,128]{1,0:T(8,128)(2,1)S(1)} collective-permute-done((bf16[344,128]{1,0:T(8,128)(2,1)S(1)}, bf16[344,128]{1,0:T(8,128)(2,1)S(1)}, u32[]{:S(2)}, u32[]{:S(2)}) %collective-permute-start.3) | collective-permute-done | bytes 88096 | tf_op jit(solution)/shard_map/ppermute | solution.py:345
  16.4 0.6 %shard_map.85.refs_0_ = bf16[2,64,128]{2,1,0:T(8,128)(2,1)S(1)} custom-call(bf16[2,2,16,128]{3,2,1,0:T(8,128)(2,1)S(1)} %get-tuple-element.11.refs_0_, bf16[2,2,16,128]{3,2,1,0:T(8,128)(2,1)S(1)} %collective-permute-done.refs_1_, bf16[2,2,16,128]{3,2,1,0:T(8,128)(2,1)S(1)} %collective-permute-done.1.refs_2_, ...), custom_call_target="tpu_custom_call" | custom-call | flops 10000000000 | bytes 1048576 | tf_op jit(solution)/shard_map/pallas_call | solution.py:346
  17.1 0.1 collective-permute-start.6
  17.1 1.7 %collective-permute-start.5 = (bf16[2,64,128]{2,1,0:T(8,128)(2,1)S(1)}, bf16[2,64,128]{2,1,0:T(8,128)(2,1)S(1)}, u32[]{:S(2)}, u32[]{:S(2)}) collective-permute-start(bf16[2,64,128]{2,1,0:T(8,128)(2,1)S(1)} %shard_map.85.refs_0_), channel_id=1, source_target_pairs={{0,4},{2,6},{4,0},{6,2},{8,12},{10,14},{12,8},{14,10},{1,5},{3,7},... | collective-permute-start | bytes 98312 | tf_op jit(solution)/shard_map/ppermute | solution.py:271
  18.9 1.7 %collective-permute-start.4 = (bf16[2,64,128]{2,1,0:T(8,128)(2,1)S(1)}, bf16[2,64,128]{2,1,0:T(8,128)(2,1)S(1)}, u32[]{:S(2)}, u32[]{:S(2)}) collective-permute-start(bf16[2,64,128]{2,1,0:T(8,128)(2,1)S(1)} %shard_map.85.refs_0_), channel_id=1, source_target_pairs={{0,2},{2,0},{4,6},{6,4},{8,10},{10,8},{12,14},{14,12},{1,3},{3,1},... | collective-permute-start | bytes 98312 | tf_op jit(solution)/shard_map/ppermute | solution.py:271
  20.6 1.3 %collective-permute-done.6.refs_3_ = bf16[2,64,128]{2,1,0:T(8,128)(2,1)S(1)} collective-permute-done((bf16[2,64,128]{2,1,0:T(8,128)(2,1)S(1)}, bf16[2,64,128]{2,1,0:T(8,128)(2,1)S(1)}, u32[]{:S(2)}, u32[]{:S(2)}) %collective-permute-start.6) | collective-permute-done | bytes 32800 | tf_op jit(solution)/shard_map/ppermute | solution.py:271
  21.9 0.0 collective-permute-done.5.refs_2_
  21.9 0.8 %collective-permute-done.4.refs_1_ = bf16[2,64,128]{2,1,0:T(8,128)(2,1)S(1)} collective-permute-done((bf16[2,64,128]{2,1,0:T(8,128)(2,1)S(1)}, bf16[2,64,128]{2,1,0:T(8,128)(2,1)S(1)}, u32[]{:S(2)}, u32[]{:S(2)}) %collective-permute-start.4) | collective-permute-done | bytes 32800 | tf_op jit(solution)/shard_map/ppermute | solution.py:271
  22.8 0.0 slice-done
  22.8 2.3 %shard_map.86 = (f32[2,4,1024]{2,1,0:T(4,128)S(1)}, f32[2,4,1024]{2,1,0:T(4,128)S(1)}) custom-call(bf16[2,64,128]{2,1,0:T(8,128)(2,1)S(1)} %shard_map.85.refs_0_, bf16[2,64,128]{2,1,0:T(8,128)(2,1)S(1)} %collective-permute-done.4.refs_1_, bf16[2,64,128]{2,1,0:T(8,128)(2,1)S(1)} %collective-permute-done.5.refs_2_, ...), custom_call_target="tpu_custom_call" | custom-call | tf_op jit(solution)/shard_map/pallas_call | solution.py:356
  25.1 0.0 collective-permute-start.7
  25.1 1.2 %collective-permute-done.7 = f32[2,4,1024]{2,1,0:T(4,128)S(1)} collective-permute-done((f32[2,4,1024]{2,1,0:T(4,128)S(1)}, f32[2,4,1024]{2,1,0:T(4,128)S(1)}, u32[]{:S(2)}, u32[]{:S(2)}) %collective-permute-start.7) | collective-permute-done | bytes 32800 | tf_op jit(solution)/shard_map/ppermute | solution.py:364
  26.3 0.6 %add_convert_fusion = bf16[2,4,1024]{2,1,0:T(4,128)(2,1)} fusion(f32[2,4,1024]{2,1,0:T(4,128)S(1)} %get-tuple-element.15, f32[2,4,1024]{2,1,0:T(4,128)S(1)} %collective-permute-done.7), kind=kLoop, calls=%fused_computation | loop fusion | flops 16384 | bytes 81920 | tf_op jit(solution)/shard_map/convert_element_type | solution.py:365
  (8 shorter events, 0.0 us)
Async XLA Ops:
  0.8 6.0 %collective-permute-start = (bf16[2,2,16,128]{3,2,1,0:T(8,128)(2,1)S(1)}, bf16[2,2,16,128]{3,2,1,0:T(8,128)(2,1)S(1)}, u32[]{:S(2)}, u32[]{:S(2)}) collective-permute-start(bf16[2,2,16,128]{3,2,1,0:T(8,128)(2,1)S(1)} %get-tuple-element.12), channel_id=1, source_target_pairs={{0,2},{2,0},{4,6},{6,4},{8,10},{10,8},{12,14},{14,12},{1,3},{3,1},... | collective-permute-start | bytes 49160 | tf_op jit(solution)/shard_map/ppermute | solution.py:271
  3.9 3.8 %collective-permute-start.1 = (bf16[2,2,16,128]{3,2,1,0:T(8,128)(2,1)S(1)}, bf16[2,2,16,128]{3,2,1,0:T(8,128)(2,1)S(1)}, u32[]{:S(2)}, u32[]{:S(2)}) collective-permute-start(bf16[2,2,16,128]{3,2,1,0:T(8,128)(2,1)S(1)} %get-tuple-element.13), channel_id=1, source_target_pairs={{0,4},{2,6},{4,0},{6,2},{8,12},{10,14},{12,8},{14,10},{1,5},{3,7},... | collective-permute-start | bytes 49160 | tf_op jit(solution)/shard_map/ppermute | solution.py:271
  5.4 4.6 %collective-permute-start.2 = (bf16[2,2,16,128]{3,2,1,0:T(8,128)(2,1)S(1)}, bf16[2,2,16,128]{3,2,1,0:T(8,128)(2,1)S(1)}, u32[]{:S(2)}, u32[]{:S(2)}) collective-permute-start(bf16[2,2,16,128]{3,2,1,0:T(8,128)(2,1)S(1)} %get-tuple-element.14), channel_id=1, source_target_pairs={{0,6},{2,4},{4,2},{6,0},{8,14},{10,12},{12,10},{14,8},{1,7},{3,5},... | collective-permute-start | bytes 49160 | tf_op jit(solution)/shard_map/ppermute | solution.py:271
  10.1 12.7 %slice-start = ((s8[16777216]{0:T(1024)(128)(4,1)}), s8[4194304]{0:T(1024)(128)(4,1)S(1)}, s32[]{:S(2)}) async-start(s8[16777216]{0:T(1024)(128)(4,1)} %bitcast.6), calls=%async_computation | async-start | bytes 8388608
  10.1 12.7 %slice-start.1 = ((s8[16777216]{0:T(1024)(128)(4,1)}), s8[4194304]{0:T(1024)(128)(4,1)S(1)}, s32[]{:S(2)}) async-start(s8[16777216]{0:T(1024)(128)(4,1)} %bitcast.6), calls=%async_computation.1 | async-start | bytes 8388608
  10.1 12.7 %slice-start.2 = ((s8[16777216]{0:T(1024)(128)(4,1)}), s8[4194304]{0:T(1024)(128)(4,1)S(1)}, s32[]{:S(2)}) async-start(s8[16777216]{0:T(1024)(128)(4,1)} %bitcast.6), calls=%async_computation.2 | async-start | bytes 8388608
  10.1 12.7 %slice-start.3 = ((s8[16777216]{0:T(1024)(128)(4,1)}), s8[4194304]{0:T(1024)(128)(4,1)S(1)}, s32[]{:S(2)}) async-start(s8[16777216]{0:T(1024)(128)(4,1)} %bitcast.6), calls=%async_computation.3 | async-start | bytes 8388608
  10.1 6.3 %collective-permute-start.3 = (bf16[344,128]{1,0:T(8,128)(2,1)S(1)}, bf16[344,128]{1,0:T(8,128)(2,1)S(1)}, u32[]{:S(2)}, u32[]{:S(2)}) collective-permute-start(bf16[344,128]{1,0:T(8,128)(2,1)S(1)} %shard_map.84), channel_id=1, source_target_pairs={{0,8},{2,10},{4,12},{6,14},{8,0},{10,2},{12,4},{14,6},{1,9},{3,11}... | collective-permute-start | bytes 264200 | tf_op jit(solution)/shard_map/ppermute | solution.py:345
  17.1 4.9 %collective-permute-start.6 = (bf16[2,64,128]{2,1,0:T(8,128)(2,1)S(1)}, bf16[2,64,128]{2,1,0:T(8,128)(2,1)S(1)}, u32[]{:S(2)}, u32[]{:S(2)}) collective-permute-start(bf16[2,64,128]{2,1,0:T(8,128)(2,1)S(1)} %shard_map.85.refs_0_), channel_id=1, source_target_pairs={{0,6},{2,4},{4,2},{6,0},{8,14},{10,12},{12,10},{14,8},{1,7},{3,5},... | collective-permute-start | bytes 98312 | tf_op jit(solution)/shard_map/ppermute | solution.py:271
  17.1 4.8 %collective-permute-start.5 = (bf16[2,64,128]{2,1,0:T(8,128)(2,1)S(1)}, bf16[2,64,128]{2,1,0:T(8,128)(2,1)S(1)}, u32[]{:S(2)}, u32[]{:S(2)}) collective-permute-start(bf16[2,64,128]{2,1,0:T(8,128)(2,1)S(1)} %shard_map.85.refs_0_), channel_id=1, source_target_pairs={{0,4},{2,6},{4,0},{6,2},{8,12},{10,14},{12,8},{14,10},{1,5},{3,7},... | collective-permute-start | bytes 98312 | tf_op jit(solution)/shard_map/ppermute | solution.py:271
  18.9 3.9 %collective-permute-start.4 = (bf16[2,64,128]{2,1,0:T(8,128)(2,1)S(1)}, bf16[2,64,128]{2,1,0:T(8,128)(2,1)S(1)}, u32[]{:S(2)}, u32[]{:S(2)}) collective-permute-start(bf16[2,64,128]{2,1,0:T(8,128)(2,1)S(1)} %shard_map.85.refs_0_), channel_id=1, source_target_pairs={{0,2},{2,0},{4,6},{6,4},{8,10},{10,8},{12,14},{14,12},{1,3},{3,1},... | collective-permute-start | bytes 98312 | tf_op jit(solution)/shard_map/ppermute | solution.py:271
  25.1 1.2 %collective-permute-start.7 = (f32[2,4,1024]{2,1,0:T(4,128)S(1)}, f32[2,4,1024]{2,1,0:T(4,128)S(1)}, u32[]{:S(2)}, u32[]{:S(2)}) collective-permute-start(f32[2,4,1024]{2,1,0:T(4,128)S(1)} %get-tuple-element.16), channel_id=1, source_target_pairs={{0,1},{1,0},{2,3},{3,2},{4,5},{5,4},{6,7},{7,6},{8,9},{9,8},{10,11... | collective-permute-start | bytes 98312 | tf_op jit(solution)/shard_map/ppermute | solution.py:364

commit v7 on v6

--- a/solution.py
+++ b/solution.py
@@ -187,9 +187,8 @@
     per_block = 4 * block
     sources = 2 * pairs
     cached = sources * block
-    shape = (query_rows, cached + groups)
-    group = lax.broadcasted_iota(jnp.int32, shape, 0) // (query_rows // groups)
-    column = lax.broadcasted_iota(jnp.int32, shape, 1)
+    group = lax.broadcasted_iota(jnp.int32, (query_rows, 1), 0) // (query_rows // groups)
+    column = lax.broadcasted_iota(jnp.int32, (1, cached + groups), 1)
     within = column % block
     column_group = (within // (positions * kv_heads)) * kv_heads + within % kv_heads
     source = column // block
@@ -354,7 +353,7 @@
     contexts = exchange([contexts] * pairs)
     part = jax.ShapeDtypeStruct((layers, sequences // 2, columns), f32)
     mine, other = pl.pallas_call(
-        functools.partial(pair_project_kernel, pairs, layers, 4 * depth),
+        functools.partial(pair_project_kernel, pairs, layers, 16 * depth),
         out_shape=(part, part),
         in_specs=[VMEM] * (pairs + 1),
         out_specs=(VMEM, VMEM),

time: 27.2 us -> 27.2 us (level)
  no operation moved by 1% of the time
where the time goes in v7:
time: 27.2 us; the launch traced here: 26.9 us
  starting transfers between devices  11 us (40%)
  waiting for transfers between devices  10.1 us (37%)
  Pallas kernels  4.46 us (16%)
  between operations  0.74 us (3%)
  other arithmetic  0.62 us (2%)
    ppermute x6, starting transfers between devices, exchange(): lax.ppermute(blocks[k], 'seq', [(i, i ^ k) for i in range(count)])  8.16 us
    ppermute x6, waiting for transfers between devices, exchange(): lax.ppermute(blocks[k], 'seq', [(i, i ^ k) for i in range(count)])  5.4 us
    ppermute x1, waiting for transfers between devices, by_pairs(): lax.ppermute(packed, 'seq', [(i, i ^ pairs) for i in range(sequences)])  3.47 us
    ppermute x1, starting transfers between devices, by_pairs(): lax.ppermute(packed, 'seq', [(i, i ^ pairs) for i in range(sequences)])  2.83 us
    pallas_call x1, Pallas kernels, by_pairs(): pl.pallas_call(functools.partial(pair_project_kernel, pairs, layers, 16 *...  2.28 us
    ppermute x1, waiting for transfers between devices, by_pairs(): arrived = lax.ppermute(other, 'head', [(0, 1), (1, 0)])  1.22 us
    pallas_call x1, Pallas kernels, by_pairs(): pl.pallas_call(functools.partial(stage_kernel, pairs), out_shape=[block_s...  0.82 us
    pallas_call x1, Pallas kernels, by_pairs(): pl.pallas_call(own_rows_kernel, out_shape=jax.ShapeDtypeStruct((side_rows...  0.75 us
  transfers between devices with their start and end apart: 8, of which 6 were waited for; matrix products, arithmetic and copies ran while one was open for 0% of the time, Pallas kernels for 3%

profile of v7, /device:TPU:0, one launch (start us, length us, event | category | flops | bytes accessed | tf_op | source)
XLA Modules:
  0.0 26.9 jit_solution(17920968188166748973)
XLA Ops:
  0.0 0.8 %shard_map.82 = (bf16[2,2,16,128]{3,2,1,0:T(8,128)(2,1)S(1)}, bf16[2,2,16,128]{3,2,1,0:T(8,128)(2,1)S(1)}, bf16[2,2,16,128]{3,2,1,0:T(8,128)(2,1)S(1)}, bf16[2,2,16,128]{3,2,1,0:T(8,128)(2,1)S(1)}) custom-call(s32[8]{0:T(128)} %slot_hbm.1, bf16[2,8,8,128]{3,2,1,0:T(8,128)(2,1)} %bitcast.8, bf16[2,8,8,128]{3,2,1,0:T(8,128)(2,1)} %bitcast.9), custom_call_target="tpu_custom_call" | custom-call | flops 10000000000 | bytes 1048576 | tf_op jit(solution)/shard_map/pallas_call | solution.py:303
  0.8 3.0 %collective-permute-start = (bf16[2,2,16,128]{3,2,1,0:T(8,128)(2,1)S(1)}, bf16[2,2,16,128]{3,2,1,0:T(8,128)(2,1)S(1)}, u32[]{:S(2)}, u32[]{:S(2)}) collective-permute-start(bf16[2,2,16,128]{3,2,1,0:T(8,128)(2,1)S(1)} %get-tuple-element.12), channel_id=1, source_target_pairs={{0,2},{2,0},{4,6},{6,4},{8,10},{10,8},{12,14},{14,12},{1,3},{3,1},... | collective-permute-start | bytes 49160 | tf_op jit(solution)/shard_map/ppermute | solution.py:270
  3.9 1.6 %collective-permute-start.1 = (bf16[2,2,16,128]{3,2,1,0:T(8,128)(2,1)S(1)}, bf16[2,2,16,128]{3,2,1,0:T(8,128)(2,1)S(1)}, u32[]{:S(2)}, u32[]{:S(2)}) collective-permute-start(bf16[2,2,16,128]{3,2,1,0:T(8,128)(2,1)S(1)} %get-tuple-element.13), channel_id=1, source_target_pairs={{0,4},{2,6},{4,0},{6,2},{8,12},{10,14},{12,8},{14,10},{1,5},{3,7},... | collective-permute-start | bytes 49160 | tf_op jit(solution)/shard_map/ppermute | solution.py:270
  5.4 0.0 collective-permute-start.2
  5.4 0.7 %shard_map.83.refs_4_ = bf16[80,128]{1,0:T(8,128)(2,1)S(1)} custom-call(bf16[64,128]{1,0:T(8,128)(2,1)} %bitcast.10, bf16[8,128]{1,0:T(8,128)(2,1)} %bitcast.11, bf16[8,128]{1,0:T(8,128)(2,1)} %bitcast.12), custom_call_target="tpu_custom_call" | custom-call | flops 10000000000 | bytes 1048576 | tf_op jit(solution)/shard_map/pallas_call | solution.py:320
  6.8 0.0 collective-permute-done.refs_1_
  6.9 0.8 %collective-permute-done.1.refs_2_ = bf16[2,2,16,128]{3,2,1,0:T(8,128)(2,1)S(1)} collective-permute-done((bf16[2,2,16,128]{3,2,1,0:T(8,128)(2,1)S(1)}, bf16[2,2,16,128]{3,2,1,0:T(8,128)(2,1)S(1)}, u32[]{:S(2)}, u32[]{:S(2)}) %collective-permute-start.1) | collective-permute-done | bytes 16416 | tf_op jit(solution)/shard_map/ppermute | solution.py:270
  7.6 2.4 %collective-permute-done.2.refs_3_ = bf16[2,2,16,128]{3,2,1,0:T(8,128)(2,1)S(1)} collective-permute-done((bf16[2,2,16,128]{3,2,1,0:T(8,128)(2,1)S(1)}, bf16[2,2,16,128]{3,2,1,0:T(8,128)(2,1)S(1)}, u32[]{:S(2)}, u32[]{:S(2)}) %collective-permute-start.2) | collective-permute-done | bytes 16416 | tf_op jit(solution)/shard_map/ppermute | solution.py:270
  10.1 0.0 slice-start.2
  10.1 0.0 slice-start.3
  10.1 2.8 %collective-permute-start.3 = (bf16[344,128]{1,0:T(8,128)(2,1)S(1)}, bf16[344,128]{1,0:T(8,128)(2,1)S(1)}, u32[]{:S(2)}, u32[]{:S(2)}) collective-permute-start(bf16[344,128]{1,0:T(8,128)(2,1)S(1)} %shard_map.84), channel_id=1, source_target_pairs={{0,8},{2,10},{4,12},{6,14},{8,0},{10,2},{12,4},{14,6},{1,9},{3,11}... | collective-permute-start | bytes 264200 | tf_op jit(solution)/shard_map/ppermute | solution.py:344
  12.9 3.5 %collective-permute-done.3.refs_6_ = bf16[344,128]{1,0:T(8,128)(2,1)S(1)} collective-permute-done((bf16[344,128]{1,0:T(8,128)(2,1)S(1)}, bf16[344,128]{1,0:T(8,128)(2,1)S(1)}, u32[]{:S(2)}, u32[]{:S(2)}) %collective-permute-start.3) | collective-permute-done | bytes 88096 | tf_op jit(solution)/shard_map/ppermute | solution.py:344
  16.4 0.6 %shard_map.85.refs_0_ = bf16[2,64,128]{2,1,0:T(8,128)(2,1)S(1)} custom-call(bf16[2,2,16,128]{3,2,1,0:T(8,128)(2,1)S(1)} %get-tuple-element.11.refs_0_, bf16[2,2,16,128]{3,2,1,0:T(8,128)(2,1)S(1)} %collective-permute-done.refs_1_, bf16[2,2,16,128]{3,2,1,0:T(8,128)(2,1)S(1)} %collective-permute-done.1.refs_2_, ...), custom_call_target="tpu_custom_call" | custom-call | flops 10000000000 | bytes 1048576 | tf_op jit(solution)/shard_map/pallas_call | solution.py:345
  17.0 0.1 collective-permute-start.6
  17.1 1.7 %collective-permute-start.5 = (bf16[2,64,128]{2,1,0:T(8,128)(2,1)S(1)}, bf16[2,64,128]{2,1,0:T(8,128)(2,1)S(1)}, u32[]{:S(2)}, u32[]{:S(2)}) collective-permute-start(bf16[2,64,128]{2,1,0:T(8,128)(2,1)S(1)} %shard_map.85.refs_0_), channel_id=1, source_target_pairs={{0,4},{2,6},{4,0},{6,2},{8,12},{10,14},{12,8},{14,10},{1,5},{3,7},... | collective-permute-start | bytes 98312 | tf_op jit(solution)/shard_map/ppermute | solution.py:270
  18.9 1.7 %collective-permute-start.4 = (bf16[2,64,128]{2,1,0:T(8,128)(2,1)S(1)}, bf16[2,64,128]{2,1,0:T(8,128)(2,1)S(1)}, u32[]{:S(2)}, u32[]{:S(2)}) collective-permute-start(bf16[2,64,128]{2,1,0:T(8,128)(2,1)S(1)} %shard_map.85.refs_0_), channel_id=1, source_target_pairs={{0,2},{2,0},{4,6},{6,4},{8,10},{10,8},{12,14},{14,12},{1,3},{3,1},... | collective-permute-start | bytes 98312 | tf_op jit(solution)/shard_map/ppermute | solution.py:270
  20.6 1.3 %collective-permute-done.6.refs_3_ = bf16[2,64,128]{2,1,0:T(8,128)(2,1)S(1)} collective-permute-done((bf16[2,64,128]{2,1,0:T(8,128)(2,1)S(1)}, bf16[2,64,128]{2,1,0:T(8,128)(2,1)S(1)}, u32[]{:S(2)}, u32[]{:S(2)}) %collective-permute-start.6) | collective-permute-done | bytes 32800 | tf_op jit(solution)/shard_map/ppermute | solution.py:270
  21.9 0.0 collective-permute-done.5.refs_2_
  21.9 0.8 %collective-permute-done.4.refs_1_ = bf16[2,64,128]{2,1,0:T(8,128)(2,1)S(1)} collective-permute-done((bf16[2,64,128]{2,1,0:T(8,128)(2,1)S(1)}, bf16[2,64,128]{2,1,0:T(8,128)(2,1)S(1)}, u32[]{:S(2)}, u32[]{:S(2)}) %collective-permute-start.4) | collective-permute-done | bytes 32800 | tf_op jit(solution)/shard_map/ppermute | solution.py:270
  22.8 0.0 slice-done
  22.8 2.3 %shard_map.86 = (f32[2,4,1024]{2,1,0:T(4,128)S(1)}, f32[2,4,1024]{2,1,0:T(4,128)S(1)}) custom-call(bf16[2,64,128]{2,1,0:T(8,128)(2,1)S(1)} %shard_map.85.refs_0_, bf16[2,64,128]{2,1,0:T(8,128)(2,1)S(1)} %collective-permute-done.4.refs_1_, bf16[2,64,128]{2,1,0:T(8,128)(2,1)S(1)} %collective-permute-done.5.refs_2_, ...), custom_call_target="tpu_custom_call" | custom-call | tf_op jit(solution)/shard_map/pallas_call | solution.py:355
  25.1 0.0 collective-permute-start.7
  25.1 1.2 %collective-permute-done.7 = f32[2,4,1024]{2,1,0:T(4,128)S(1)} collective-permute-done((f32[2,4,1024]{2,1,0:T(4,128)S(1)}, f32[2,4,1024]{2,1,0:T(4,128)S(1)}, u32[]{:S(2)}, u32[]{:S(2)}) %collective-permute-start.7) | collective-permute-done | bytes 32800 | tf_op jit(solution)/shard_map/ppermute | solution.py:363
  26.3 0.6 %add_convert_fusion = bf16[2,4,1024]{2,1,0:T(4,128)(2,1)} fusion(f32[2,4,1024]{2,1,0:T(4,128)S(1)} %get-tuple-element.15, f32[2,4,1024]{2,1,0:T(4,128)S(1)} %collective-permute-done.7), kind=kLoop, calls=%fused_computation | loop fusion | flops 16384 | bytes 81920 | tf_op jit(solution)/shard_map/convert_element_type | solution.py:364
  (8 shorter events, 0.0 us)
Async XLA Ops:
  0.8 6.0 %collective-permute-start = (bf16[2,2,16,128]{3,2,1,0:T(8,128)(2,1)S(1)}, bf16[2,2,16,128]{3,2,1,0:T(8,128)(2,1)S(1)}, u32[]{:S(2)}, u32[]{:S(2)}) collective-permute-start(bf16[2,2,16,128]{3,2,1,0:T(8,128)(2,1)S(1)} %get-tuple-element.12), channel_id=1, source_target_pairs={{0,2},{2,0},{4,6},{6,4},{8,10},{10,8},{12,14},{14,12},{1,3},{3,1},... | collective-permute-start | bytes 49160 | tf_op jit(solution)/shard_map/ppermute | solution.py:270
  3.9 3.8 %collective-permute-start.1 = (bf16[2,2,16,128]{3,2,1,0:T(8,128)(2,1)S(1)}, bf16[2,2,16,128]{3,2,1,0:T(8,128)(2,1)S(1)}, u32[]{:S(2)}, u32[]{:S(2)}) collective-permute-start(bf16[2,2,16,128]{3,2,1,0:T(8,128)(2,1)S(1)} %get-tuple-element.13), channel_id=1, source_target_pairs={{0,4},{2,6},{4,0},{6,2},{8,12},{10,14},{12,8},{14,10},{1,5},{3,7},... | collective-permute-start | bytes 49160 | tf_op jit(solution)/shard_map/ppermute | solution.py:270
  5.4 4.6 %collective-permute-start.2 = (bf16[2,2,16,128]{3,2,1,0:T(8,128)(2,1)S(1)}, bf16[2,2,16,128]{3,2,1,0:T(8,128)(2,1)S(1)}, u32[]{:S(2)}, u32[]{:S(2)}) collective-permute-start(bf16[2,2,16,128]{3,2,1,0:T(8,128)(2,1)S(1)} %get-tuple-element.14), channel_id=1, source_target_pairs={{0,6},{2,4},{4,2},{6,0},{8,14},{10,12},{12,10},{14,8},{1,7},{3,5},... | collective-permute-start | bytes 49160 | tf_op jit(solution)/shard_map/ppermute | solution.py:270
  10.1 12.7 %slice-start = ((s8[16777216]{0:T(1024)(128)(4,1)}), s8[4194304]{0:T(1024)(128)(4,1)S(1)}, s32[]{:S(2)}) async-start(s8[16777216]{0:T(1024)(128)(4,1)} %bitcast.6), calls=%async_computation | async-start | bytes 8388608
  10.1 12.7 %slice-start.1 = ((s8[16777216]{0:T(1024)(128)(4,1)}), s8[4194304]{0:T(1024)(128)(4,1)S(1)}, s32[]{:S(2)}) async-start(s8[16777216]{0:T(1024)(128)(4,1)} %bitcast.6), calls=%async_computation.1 | async-start | bytes 8388608
  10.1 12.7 %slice-start.2 = ((s8[16777216]{0:T(1024)(128)(4,1)}), s8[4194304]{0:T(1024)(128)(4,1)S(1)}, s32[]{:S(2)}) async-start(s8[16777216]{0:T(1024)(128)(4,1)} %bitcast.6), calls=%async_computation.2 | async-start | bytes 8388608
  10.1 12.7 %slice-start.3 = ((s8[16777216]{0:T(1024)(128)(4,1)}), s8[4194304]{0:T(1024)(128)(4,1)S(1)}, s32[]{:S(2)}) async-start(s8[16777216]{0:T(1024)(128)(4,1)} %bitcast.6), calls=%async_computation.3 | async-start | bytes 8388608
  10.1 6.3 %collective-permute-start.3 = (bf16[344,128]{1,0:T(8,128)(2,1)S(1)}, bf16[344,128]{1,0:T(8,128)(2,1)S(1)}, u32[]{:S(2)}, u32[]{:S(2)}) collective-permute-start(bf16[344,128]{1,0:T(8,128)(2,1)S(1)} %shard_map.84), channel_id=1, source_target_pairs={{0,8},{2,10},{4,12},{6,14},{8,0},{10,2},{12,4},{14,6},{1,9},{3,11}... | collective-permute-start | bytes 264200 | tf_op jit(solution)/shard_map/ppermute | solution.py:344
  17.0 4.9 %collective-permute-start.6 = (bf16[2,64,128]{2,1,0:T(8,128)(2,1)S(1)}, bf16[2,64,128]{2,1,0:T(8,128)(2,1)S(1)}, u32[]{:S(2)}, u32[]{:S(2)}) collective-permute-start(bf16[2,64,128]{2,1,0:T(8,128)(2,1)S(1)} %shard_map.85.refs_0_), channel_id=1, source_target_pairs={{0,6},{2,4},{4,2},{6,0},{8,14},{10,12},{12,10},{14,8},{1,7},{3,5},... | collective-permute-start | bytes 98312 | tf_op jit(solution)/shard_map/ppermute | solution.py:270
  17.1 4.8 %collective-permute-start.5 = (bf16[2,64,128]{2,1,0:T(8,128)(2,1)S(1)}, bf16[2,64,128]{2,1,0:T(8,128)(2,1)S(1)}, u32[]{:S(2)}, u32[]{:S(2)}) collective-permute-start(bf16[2,64,128]{2,1,0:T(8,128)(2,1)S(1)} %shard_map.85.refs_0_), channel_id=1, source_target_pairs={{0,4},{2,6},{4,0},{6,2},{8,12},{10,14},{12,8},{14,10},{1,5},{3,7},... | collective-permute-start | bytes 98312 | tf_op jit(solution)/shard_map/ppermute | solution.py:270
  18.9 3.9 %collective-permute-start.4 = (bf16[2,64,128]{2,1,0:T(8,128)(2,1)S(1)}, bf16[2,64,128]{2,1,0:T(8,128)(2,1)S(1)}, u32[]{:S(2)}, u32[]{:S(2)}) collective-permute-start(bf16[2,64,128]{2,1,0:T(8,128)(2,1)S(1)} %shard_map.85.refs_0_), channel_id=1, source_target_pairs={{0,2},{2,0},{4,6},{6,4},{8,10},{10,8},{12,14},{14,12},{1,3},{3,1},... | collective-permute-start | bytes 98312 | tf_op jit(solution)/shard_map/ppermute | solution.py:270
  25.1 1.2 %collective-permute-start.7 = (f32[2,4,1024]{2,1,0:T(4,128)S(1)}, f32[2,4,1024]{2,1,0:T(4,128)S(1)}, u32[]{:S(2)}, u32[]{:S(2)}) collective-permute-start(f32[2,4,1024]{2,1,0:T(4,128)S(1)} %get-tuple-element.16), channel_id=1, source_target_pairs={{0,1},{1,0},{2,3},{3,2},{4,5},{5,4},{6,7},{7,6},{8,9},{9,8},{10,11... | collective-permute-start | bytes 98312 | tf_op jit(solution)/shard_map/ppermute | solution.py:363
